TPU v7x, 32 devices: a whole 2x2x4 slice. The times are simulated.
32 devices in a mesh: dp: 2 (over x), tp: 4 (over z), sp: 4 (over y, core).
Axes of the slice: x: 2, y: 2, z: 4, core: 2. Of those that a mesh axis runs over, the one named last changes fastest.
Arguments:
- hidden: bfloat16 [512, 6144], P('dp'), parts along dimension 0
- ln_gain: bfloat16 [6144], replicated
- ln_bias: bfloat16 [6144], replicated
- w_q: bfloat16 [6144, 6144], P(None, 'tp')
- w_k: bfloat16 [6144, 1024], P(None, 'tp')
- w_v: bfloat16 [6144, 1024], P(None, 'tp')
- w_o: bfloat16 [6144, 6144], P('tp')
- k_cache: bfloat16 [512, 512, 8, 128], P('dp', 'sp', 'tp'), parts along dimension 0
- v_cache: bfloat16 [512, 512, 8, 128], P('dp', 'sp', 'tp'), parts along dimension 0
- lengths: int32 [512], P('dp'), parts along dimension 0
Outputs:
- output 1: bfloat16 [512, 6144], P('dp'), parts along dimension 0
- output 2: bfloat16 [512, 8, 128], P('dp', 'tp'), parts along dimension 0
- output 3: bfloat16 [512, 8, 128], P('dp', 'tp'), parts along dimension 0
There are 2 independent parts. A program takes and returns all parts, laid end to end along the dimension named above; an argument that names none is the same for every part.
All inputs are finite; a program needn't handle non-finite values.
Results may differ from a plain program's by a relative error of at most 0.00411564.
Values sent between devices are 32-bit elements.
A program may use at most 1 GiB of HBM per device.

v0:
```python
import jax
import jax.numpy as jnp
from jax import lax
from jax.sharding import PartitionSpec as P, NamedSharding


def norm_one_plus(hidden, ln_gain, ln_bias):
    wide = hidden.astype(jnp.float32)
    row_mean = jnp.mean(wide, axis=-1, keepdims=True)
    centred = wide - row_mean
    row_var = jnp.mean(centred * centred, axis=-1, keepdims=True)
    scaled = centred * lax.rsqrt(row_var + 1e-5)
    return (scaled * (1.0 + ln_gain.astype(jnp.float32)) + ln_bias.astype(jnp.float32)).astype(jnp.bfloat16)


def rotate_first(head_vecs, rot_pos, rot_dim):
    half_rot = rot_dim // 2
    inv_freq = 10000.0 ** (-2.0 * jnp.arange(half_rot, dtype=jnp.float32) / rot_dim)
    rot_angle = rot_pos.astype(jnp.float32)[..., None] * inv_freq
    cos_part = jnp.cos(rot_angle)
    sin_part = jnp.sin(rot_angle)
    lead_part = head_vecs[..., :half_rot]
    tail_part = head_vecs[..., half_rot:rot_dim]
    return jnp.concatenate([lead_part * cos_part - tail_part * sin_part, tail_part * cos_part + lead_part * sin_part, head_vecs[..., rot_dim:]], axis=-1)


def solution(mesh):
    def local_step(hidden, ln_gain, ln_bias, w_q, w_k, w_v, w_o, k_cache, v_cache, lengths):
        batch_rows, seq_local, kv_local, head_dim = k_cache.shape
        group_size = w_q.shape[1] // (head_dim * kv_local)
        rot_dim = head_dim // 2
        score_scale = head_dim ** -0.5
        normed = norm_one_plus(hidden, ln_gain, ln_bias)
        q_proj = jnp.dot(normed, w_q, preferred_element_type=jnp.float32).reshape(batch_rows, kv_local, group_size, head_dim)
        queries = rotate_first(q_proj, lengths[:, None, None], rot_dim).astype(jnp.bfloat16)
        k_proj = jnp.dot(normed, w_k, preferred_element_type=jnp.float32).reshape(batch_rows, kv_local, head_dim)
        k_new = rotate_first(k_proj, lengths[:, None], rot_dim).astype(jnp.bfloat16)
        v_new = jnp.dot(normed, w_v, preferred_element_type=jnp.float32).astype(jnp.bfloat16).reshape(batch_rows, kv_local, head_dim)
        block_index = lax.axis_index('sp')
        positions = block_index * seq_local + jnp.arange(seq_local)
        valid = positions[None, :] < lengths[:, None]
        scores = jnp.einsum('bkgd,bskd->bkgs', queries, k_cache, preferred_element_type=jnp.float32) * score_scale
        scores = jnp.where(valid[:, None, None, :], scores, -jnp.inf)
        owner = (lengths // seq_local) == block_index
        self_score = jnp.einsum('clhe,cle->clh', queries, k_new, preferred_element_type=jnp.float32) * score_scale
        self_score = jnp.where(owner[:, None, None], self_score, -jnp.inf)
        block_max = jnp.maximum(jnp.max(scores, axis=-1), self_score)
        safe_max = jnp.where(jnp.isfinite(block_max), block_max, 0.0)
        weights = jnp.exp(scores - safe_max[..., None])
        self_weight = jnp.exp(self_score - safe_max)
        weight_sum = jnp.sum(weights, axis=-1) + self_weight
        weighted = jnp.einsum('bkgs,bskd->bkgd', weights.astype(jnp.bfloat16), v_cache, preferred_element_type=jnp.float32)
        weighted = weighted + self_weight[..., None] * v_new.astype(jnp.float32)[:, :, None, :]
        packed = jnp.concatenate([weighted, block_max[..., None], weight_sum[..., None]], axis=-1)
        gathered = lax.all_gather(packed, 'sp', axis=0)
        all_max = gathered[..., head_dim]
        global_max = jnp.max(all_max, axis=0)
        factor = jnp.exp(all_max - global_max)
        total = jnp.sum(gathered[..., head_dim + 1] * factor, axis=0)
        context = jnp.sum(gathered[..., :head_dim] * factor[..., None], axis=0) / total[..., None]
        context = context.astype(jnp.bfloat16).reshape(batch_rows, kv_local * group_size * head_dim)
        partial_out = jnp.dot(context, w_o, preferred_element_type=jnp.float32)
        summed = lax.psum(partial_out, 'tp')
        out = (hidden.astype(jnp.float32) + summed).astype(jnp.bfloat16)
        return out, k_new, v_new

    row_spec = P('dp', None)
    cache_spec = P('dp', 'sp', 'tp', None)
    head_spec = P('dp', 'tp', None)
    return jax.shard_map(local_step, mesh=mesh, in_specs=(row_spec, P(None), P(None), P(None, 'tp'), P(None, 'tp'), P(None, 'tp'), P('tp', None), cache_spec, cache_spec, P('dp')), out_specs=(row_spec, head_spec, head_spec), check_vma=False)
```

profile of v0, /device:TPU:0, one launch (start us, length us, event | category | flops | bytes accessed | tf_op | source)
XLA Modules:
  0.0 401.1 jit_solution(8869334463865014454)
XLA Ops:
  7.3 2.5 convert_reduce_fusion
  9.8 0.4 copy-done.2
  10.2 1.0 fusion.6
  11.2 1.5 fusion.9
  12.8 1.4 fusion.36
  14.2 0.6 slice.43
  14.9 0.7 fusion.34
  15.5 11.9 %fusion.35 = f32[256,1536]{0,1:T(8,128)S(1)} fusion(bf16[256,6144]{1,0:T(8,128)(2,1)S(1)} %fusion.9, bf16[6144,1536]{1,0:T(8,128)(2,1)} %param.13), kind=kOutput, calls=%fused_computation.69 | convolution fusion | flops 4831838208 | bytes 23592960 | tf_op jit(solution)/shard_map/dot_general | solution.py:34
  27.5 1.0 fusion.33
  28.5 0.7 broadcast_compare_fusion
  29.2 3.9 convolution_convert_fusion
  33.1 1.0 copy.132
  34.1 0.8 copy.133
  34.9 1.6 copy.168
  36.6 1.7 copy.167
  38.2 1.7 copy.166
  39.9 1.2 copy.165
  41.1 1.5 copy.164
  42.5 1.5 copy.163
  44.0 0.5 multiply_cosine_fusion
  44.6 1.4 subtract_convert_fusion.1
  46.0 0.4 subtract_convert_fusion
  46.4 0.6 fusion.46
  47.0 0.7 pad_maximum_fusion.1
  47.8 0.7 fusion.17
  48.5 12.4 %fusion.12 = (f32[256,2,6]{2,1,0:T(2,128)S(1)}, f32[256,2,6,128]{3,2,1,0:T(8,128)S(1)}) fusion(pred[256,128]{1,0:T(8,128)(4,1)S(1)} %copy-done.8, bf16[256,128,2,128]{3,2,1,0:T(2,128)(2,1)} %param.17, bf16[256,2,6,128]{3,0,2,1:T(8,128)(2,1)S(1)} %pad_maximum_fusion.1), kind=kOutput, calls=%fused_computation.20 | convolution fusion | flops 101839872 | bytes 19181568 | tf_op jit(solution)/shard_map/bkgd,bskd->bkgs/dot_general | solution.py:42
  60.9 0.3 is-finite_select_fusion
  61.3 1.4 fusion.13
  62.7 1.0 add_bitcast_fusion
  63.8 9.2 %multiply_add_fusion = f32[256,2,6,128]{3,2,1,0:T(8,128)} fusion(bf16[256,128,2,128]{3,2,1,0:T(2,128)(2,1)} %param.18, f32[256,2,6,128]{3,2,1,0:T(8,128)S(1)} %get-tuple-element.41, f32[256,2,128]{2,1,0:T(2,128)S(1)} %copy-done.9, f32[256,2,6]{2,1,0:T(2,128)S(1)} %get-tuple-element.25, f32[256,2,6]{2,1,0:T(2,128)S(1)} %is-finite_select_fusion, ...), kind=kOutput, calls=%fused_computation.17 | convolution fusion | flops 103022592 | bytes 20242432 | tf_op jit(solution)/shard_map/bkgs,bskd->bkgd/dot_general | solution.py:52
  73.0 2.4 copy.136
  75.3 0.1 copy.138
  75.4 0.1 copy.137
  75.6 1.9 pad_maximum_fusion
  77.6 50.7 %all-gather.3.cloned.1.call-done = f32[1024,2,6,130]{0,1,3,2:T(2,128)} async-done(((f32[256,2,6,130]{0,1,3,2:T(2,128)}), f32[1024,2,6,130]{0,1,3,2:T(2,128)}) %all-gather.3.cloned.1.call-update) | async-done | bytes 6389776 | tf_op jit(solution)/shard_map/all_gather | solution.py:55
  128.2 9.8 %reshape.199 = f32[4,256,2,6,130]{1,0,2,4,3:T(4,128)} reshape(f32[1024,2,6,130]{0,1,3,2:T(2,128)} %all-gather.3.cloned.1.call-done) | data formatting | bytes 12779520 | tf_op jit(solution)/shard_map/all_gather | solution.py:55
  138.0 0.9 fusion.32
  139.0 8.1 %fusion.11 = f32[256,2,6,128]{0,3,2,1:T(8,128)} fusion(f32[4,256,2,6]{1,0,3,2:T(4,128)S(1)} %exponential_bitcast_fusion, f32[4,256,2,6,130]{1,0,2,4,3:T(4,128)} %reshape.199), kind=kLoop, calls=%fused_computation.15 | loop fusion | flops 2752512 | bytes 7913472 | tf_op jit(solution)/shard_map/reduce_sum | solution.py:60
  147.1 0.8 copy.144
  147.9 2.1 copy.156
  150.1 1.6 divide_convert_fusion
  151.7 0.7 copy.145
  152.4 13.5 %fusion.37 = f32[256,6144]{1,0:T(8,128)} fusion(bf16[256,1536]{0,1:T(8,128)(2,1)S(1)} %bitcast.36, bf16[1536,6144]{1,0:T(8,128)(2,1)} %param.16), kind=kOutput, calls=%fused_computation.71 | convolution fusion | flops 4831838208 | bytes 25952256 | tf_op jit(solution)/shard_map/dot_general | solution.py:62
  166.0 0.9 copy-done.6
  166.9 0.8 copy.146
  167.6 1.2 pad_maximum_fusion.2
  168.9 219.0 %all-reduce.2.cloned.1.call-done = f32[256,6144]{1,0:T(8,128)} async-done(((f32[256,6144]{1,0:T(8,128)}), f32[256,6144]{1,0:T(8,128)}) %all-reduce.2.cloned.1.call-update) | async-done | bytes 6291472 | tf_op jit(solution)/shard_map/psum | solution.py:63
  387.9 6.4 %fusion.10 = bf16[256,6144]{1,0:T(8,128)(2,1)} fusion(f32[256,6144]{1,0:T(8,128)} %all-reduce.2.cloned.1.call-done, bf16[256,6144]{1,0:T(8,128)(2,1)} %param.10), kind=kLoop, calls=%fused_computation.13 | loop fusion | flops 4718592 | bytes 12582912 | tf_op jit(solution)/shard_map/convert_element_type | solution.py:64
  (40 shorter events, 0.4 us)
Async XLA Ops:
  7.2 5.6 %copy-start = (bf16[6144,256]{1,0:T(8,128)(2,1)S(1)}, bf16[6144,256]{1,0:T(8,128)(2,1)}, u32[]{:S(2)}) copy-start(bf16[6144,256]{1,0:T(8,128)(2,1)} %param.14) | copy-start | bytes 9437188
  7.2 121.0 %all-gather.3.cloned.1.call-start = ((), (), s32[]{:S(2)}) async-start(), calls=%async_computation.1 | async-start | bytes 7987200 | tf_op jit(solution)/shard_map/all_gather | solution.py:55
  7.2 3.0 copy-start.2
  7.3 3.9 copy-start.10
  7.3 3.9 copy-start.11
  12.8 2.7 copy-start.3
  15.5 12.9 %copy-start.12 = (s32[256]{0:T(256)S(1)}, s32[256]{0:T(256)}, u32[]{:S(2)}) copy-start(s32[256]{0:T(256)} %param.19) | copy-start | bytes 3076
  15.5 13.7 %copy-start.4 = (bf16[6144,256]{1,0:T(8,128)(2,1)S(1)}, bf16[6144,256]{1,0:T(8,128)(2,1)}, u32[]{:S(2)}) copy-start(bf16[6144,256]{1,0:T(8,128)(2,1)} %param.15) | copy-start | bytes 9437188
  44.0 2.4 copy-start.7
  44.6 2.5 copy-start.5
  46.4 2.1 copy-start.8
  60.9 2.9 copy-start.9
  77.5 310.4 %all-reduce.2.cloned.1.call-start = ((), (), s32[]{:S(2)}) async-start(), calls=%async_computation | async-start | bytes 12582912 | tf_op jit(solution)/shard_map/psum | solution.py:63
  165.9 0.9 copy-start.6
  387.9 6.4 %copy-start.1 = (bf16[6144,256]{1,0:T(8,128)(2,1)S(1)}, bf16[6144,256]{1,0:T(8,128)(2,1)}, u32[]{:S(2)}) copy-start(bf16[6144,256]{1,0:T(8,128)(2,1)} %param.14) | copy-start | bytes 9437188
Sparse Core Ops, SparseCore 0:
  77.6 50.5 all-gather.2
  166.1 221.7 all-reduce.1
where the time goes:
time: 402 us; the launch traced here: 401 us
  waiting for transfers between devices  270 us (67%)
  matrix products  53 us (13%)
  other arithmetic  32.5 us (8%)
  local copies, waits for them, and re-layouts  31.4 us (8%)
  between operations  14.4 us (4%)
    psum x1, waiting for transfers between devices, local_step(): summed = lax.psum(partial_out, 'tp')  219 us
    all_gather x1, waiting for transfers between devices, local_step(): gathered = lax.all_gather(packed, 'sp', axis=0)  50.7 us
    dot_general x1, matrix products, local_step(): partial_out = jnp.dot(context, w_o, preferred_element_type=jnp.float32)  13.5 us
    unnamed x35, local copies, waits for them, and re-layouts  13.3 us
    dot_general x1, matrix products, local_step(): jnp.einsum('bkgd,bskd->bkgs', queries, k_cache, preferred_element_type=jn...  12.4 us
    dot_general x1, matrix products, local_step(): jnp.dot(normed, w_q, preferred_element_type=jnp.float32)  11.9 us
    all_gather x1, local copies, waits for them, and re-layouts, local_step(): gathered = lax.all_gather(packed, 'sp', axis=0)  9.79 us
    dot_general x1, matrix products, local_step(): jnp.einsum('bkgs,bskd->bkgd', weights.astype(jnp.bfloat16), v_cache, pref...  9.16 us
  transfers between devices with their start and end apart: 2, of which 2 were waited for; matrix products, arithmetic and copies ran while one was open for 1% of the time, Pallas kernels for 0%

commit v1 on v0

v1 whole, which is shorter than its diff:
```python
import functools

import jax
import jax.numpy as jnp
import numpy as np
from jax import lax
from jax.experimental import pallas as pl
from jax.experimental.pallas import tpu as pltpu
from jax.sharding import PartitionSpec as P

F32 = jnp.float32
BF16 = jnp.bfloat16
MESH = pl.DeviceIdType.MESH
NEG = -0.7 * float(np.finfo(np.float32).max)
VMEM_LIMIT = 60 * 1024 * 1024
ANY = pl.BlockSpec(memory_space=pl.ANY)
VMEM = pl.BlockSpec(memory_space=pltpu.VMEM)


def qkv_kernel(gain_ref, bias_ref, cos_ref, sin_ref, x_hbm, wq_hbm, wk_hbm, wv_hbm,
               q_out, k_out, v_out, xbuf, hbuf, wbuf, qf, kf, xsem, wsem):
    rows, width = xbuf.shape
    n_q = wq_hbm.shape[1] // 256

    pltpu.make_async_copy(x_hbm, xbuf, xsem).start()

    def q_copy(i):
        return pltpu.make_async_copy(wq_hbm.at[:, pl.ds(i * 256, 256)], wbuf.at[i], wsem.at[i])

    k_copy = pltpu.make_async_copy(wk_hbm, wbuf.at[n_q], wsem.at[n_q])
    v_copy = pltpu.make_async_copy(wv_hbm, wbuf.at[n_q + 1], wsem.at[n_q + 1])
    for i in range(n_q):
        q_copy(i).start()
    k_copy.start()
    v_copy.start()

    qf[...] = jnp.zeros_like(qf)
    pltpu.make_async_copy(x_hbm, xbuf, xsem).wait()
    gain = 1.0 + gain_ref[...].astype(F32)
    bias = bias_ref[...].astype(F32)

    def norm(i, carry):
        at = pl.ds(pl.multiple_of(i * 16, 16), 16)
        wide = xbuf[at, :].astype(F32)
        mean = jnp.sum(wide, axis=-1, keepdims=True) * (1.0 / width)
        centred = wide - mean
        var = jnp.sum(centred * centred, axis=-1, keepdims=True) * (1.0 / width)
        hbuf[at, :] = (centred * lax.rsqrt(var + 1e-5) * gain + bias).astype(BF16)
        return carry

    lax.fori_loop(0, rows // 16, norm, 0)

    lane = lax.broadcasted_iota(jnp.int32, (rows, 128), 1)

    def rotate(u):
        other = jnp.where(lane < 32, -pltpu.roll(u, 96, 1), pltpu.roll(u, 32, 1))
        turned = u * cos_ref[...] + other * sin_ref[...]
        return jnp.where(lane < 64, turned, u)

    def project(i):
        return jnp.dot(hbuf[...], wbuf[i], preferred_element_type=F32)

    def q_tile(i, carry):
        q_copy(i).wait()
        prod = project(i)
        for head in range(2):
            qf[pl.ds(2 * i + head, rows, stride=16), :] = rotate(prod[:, head * 128:(head + 1) * 128])
        return carry

    lax.fori_loop(0, n_q, q_tile, 0)
    k_copy.wait()
    prod = project(n_q)
    for head in range(2):
        kf[pl.ds(head, rows, stride=2), :] = rotate(prod[:, head * 128:(head + 1) * 128])
    k_out[...] = kf[...].astype(BF16)
    v_copy.wait()
    prod = project(n_q + 1)
    for head in range(2):
        kf[pl.ds(head, rows, stride=2), :] = prod[:, head * 128:(head + 1) * 128]
    v_out[...] = kf[...].astype(BF16)
    q_out[...] = qf[...].astype(BF16)


def qkv(hidden, gain, bias, cos, sin, w_q, w_k, w_v):
    rows, width = hidden.shape
    n_tiles = w_q.shape[1] // 256 + 2
    return pl.pallas_call(
        qkv_kernel,
        out_shape=(jax.ShapeDtypeStruct((rows * 16, 128), BF16),
                   jax.ShapeDtypeStruct((rows * 2, 128), BF16),
                   jax.ShapeDtypeStruct((rows * 2, 128), BF16)),
        in_specs=[VMEM, VMEM, VMEM, VMEM, ANY, ANY, ANY, ANY],
        out_specs=(VMEM, VMEM, VMEM),
        scratch_shapes=[pltpu.VMEM((rows, width), BF16), pltpu.VMEM((rows, width), BF16),
                        pltpu.VMEM((n_tiles, width, 256), BF16),
                        pltpu.VMEM((rows * 16, 128), F32), pltpu.VMEM((rows * 2, 128), F32),
                        pltpu.SemaphoreType.DMA, pltpu.SemaphoreType.DMA((n_tiles,))],
        compiler_params=pltpu.CompilerParams(vmem_limit_bytes=VMEM_LIMIT),
        name="qkv",
    )(gain.reshape(1, width), bias.reshape(1, width), cos, sin, hidden, w_q, w_k, w_v)


def attend_kernel(len_ref, q_ref, kn_ref, vn_ref, k_ref, v_ref, o_ref, stat, *, positions, scale):
    step = pl.program_id(0)
    first = lax.axis_index("sp") * positions
    col = lax.broadcasted_iota(jnp.int32, (16, 2 * positions), 1)
    row = lax.broadcasted_iota(jnp.int32, (16, 2 * positions), 0)
    group = jnp.where(row >= 6, 1, 0)
    place = jnp.where(lax.rem(col, 2) == group, first + col // 2, 1 << 30)
    row16 = lax.broadcasted_iota(jnp.int32, (16, 16), 0)
    col16 = lax.broadcasted_iota(jnp.int32, (16, 16), 1)
    group16 = jnp.where(row16 >= 6, 1, 0)
    lane = lax.broadcasted_iota(jnp.int32, (16, 128), 1)
    pick_row = lax.broadcasted_iota(jnp.int32, (128, 16), 0)
    pick_col = lax.broadcasted_iota(jnp.int32, (128, 16), 1)
    pick = pick_col == 2 * (pick_row // 16) + jnp.where(lax.rem(pick_row, 16) >= 6, 1, 0)
    pick = jnp.where(pick, 1.0, 0.0).astype(BF16)
    nt = (((1,), (1,)), ((), ()))
    stat[...] = jnp.zeros_like(stat)
    for half in range(2):
        q8 = q_ref[half * 128:(half + 1) * 128, :]
        self8 = lax.dot_general(q8, kn_ref[half * 16:(half + 1) * 16, :], nt, preferred_element_type=F32) * scale
        v8 = jnp.dot(pick, vn_ref[half * 16:(half + 1) * 16, :], preferred_element_type=F32)
        for b in range(8):
            length = len_ref[step * 16 + half * 8 + b]
            owner = (length >= first) & (length < first + positions)
            s = lax.dot_general(q8[b * 16:(b + 1) * 16, :], k_ref[half * 8 + b], nt, preferred_element_type=F32) * scale
            s = jnp.where(place < length, s, NEG)
            mine = jnp.where(col16 == 2 * b + group16, self8[b * 16:(b + 1) * 16, :], NEG)
            own = jnp.max(mine, axis=1, keepdims=True)
            own = jnp.where(owner, own, NEG)
            top = jnp.maximum(jnp.max(s, axis=1, keepdims=True), own)
            w = jnp.exp(s - top)
            w_own = jnp.exp(own - top)
            total = jnp.sum(w, axis=1, keepdims=True) + w_own
            acc = jnp.dot(w.astype(BF16), v_ref[half * 8 + b], preferred_element_type=F32)
            acc = acc + w_own * v8[b * 16:(b + 1) * 16, :]
            o_ref[half, b * 12:(b + 1) * 12, :] = acc[:12, :]
            pair = jnp.where(lane == 0, top, total)
            stat[half, b * 12:(b + 1) * 12, :] = pair[:12, :]
        o_ref[half, 96:104, :] = jnp.transpose(stat[half])[:8, :]


def attend(lengths, q, k_new, v_new, k_cache, v_cache):
    batch, positions, kv, head = k_cache.shape
    k_rows = k_cache.reshape(batch, positions * kv, head)
    v_rows = v_cache.reshape(batch, positions * kv, head)
    steps = batch // 16
    return pl.pallas_call(
        functools.partial(attend_kernel, positions=positions, scale=head ** -0.5),
        out_shape=jax.ShapeDtypeStruct((batch // 8, 104, 128), F32),
        grid_spec=pltpu.PrefetchScalarGridSpec(
            num_scalar_prefetch=1, grid=(steps,),
            in_specs=[pl.BlockSpec((256, 128), lambda i, n: (i, 0)),
                      pl.BlockSpec((32, 128), lambda i, n: (i, 0)),
                      pl.BlockSpec((32, 128), lambda i, n: (i, 0)),
                      pl.BlockSpec((16, positions * kv, head), lambda i, n: (i, 0, 0)),
                      pl.BlockSpec((16, positions * kv, head), lambda i, n: (i, 0, 0))],
            out_specs=pl.BlockSpec((2, 104, 128), lambda i, n: (i, 0, 0)),
            scratch_shapes=[pltpu.VMEM((2, 128, 128), F32)]),
        compiler_params=pltpu.CompilerParams(vmem_limit_bytes=VMEM_LIMIT),
        name="attend",
    )(lengths, q, k_new, v_new, k_rows, v_rows)


RCH = 4
QCH = 4
NMSG = RCH * QCH


def scaled_sum(a, b):
    m_a, l_a, m_b, l_b = a[96:97, :], a[97:98, :], b[96:97, :], b[97:98, :]
    top = jnp.maximum(m_a, m_b)
    f_a, f_b = jnp.exp(m_a - top), jnp.exp(m_b - top)
    total = l_a * f_a + l_b * f_b
    r = lax.broadcasted_iota(jnp.int32, (128, 128), 0)
    turned = jnp.transpose(jnp.where(r == 0, f_a, jnp.where(r == 1, f_b, total)))
    acc = a[:96, :] * turned[:96, 0:1] + b[:96, :] * turned[:96, 1:2]
    return acc, top, total, turned[:96, 2:3]


def finish_kernel(msg, x_hbm, w_hbm, out_hbm,
                  part_y, part_o, send_y, recv_y, comb_o, ctx_t, ctx_s, ctx_r, lhs, wbuf, xbuf, prod,
                  rs_in, rs_out, fin, obuf,
                  s_py, r_py, s_po, r_po, s_y, r_y, s_c, r_c, s_w, s_x,
                  s_rs, r_rs, s_ag, r_ag, s_fy, r_fy, s_fd, r_fd, s_fe, r_fe, s_out):
    d, z, s = lax.axis_index("dp"), lax.axis_index("tp"), lax.axis_index("sp")
    y, c = s // 2, s % 2
    yo, co = 1 - y, 1 - c
    u = c * z + co * (3 - z)
    partner, across = (d, z, 2 * y + co), (d, z, 2 * yo + c)
    ahead, behind = (d, z + 2 * c - 1, s), (d, z - 2 * c + 1, s)
    half = wbuf.shape[0] * wbuf.shape[2]
    width = wbuf.shape[2]

    def remote(src, dst, send, recv, dev):
        return pltpu.make_async_remote_copy(src_ref=src, dst_ref=dst, send_sem=send, recv_sem=recv,
                                            device_id=dev, device_id_type=MESH)

    barrier = pltpu.get_barrier_semaphore()
    pl.semaphore_signal(barrier, inc=1, device_id=partner, device_id_type=MESH)
    pl.semaphore_signal(barrier, inc=1, device_id=across, device_id_type=MESH)

    @pl.when(u < 3)
    def _():
        pl.semaphore_signal(barrier, inc=1, device_id=ahead, device_id_type=MESH)

    @pl.when(u > 0)
    def _():
        pl.semaphore_signal(barrier, inc=1, device_id=behind, device_id_type=MESH)

    def w_copy(q):
        return pltpu.make_async_copy(w_hbm.at[:, pl.ds(c * half + q * width, width)], wbuf.at[q], s_w.at[q])

    x_copy = pltpu.make_async_copy(x_hbm.at[pl.ds(y * 128, 128), pl.ds(c * half, half)], xbuf, s_x)

    pl.semaphore_wait(barrier, 2 + (z + 2) // 3 + (5 - z) // 3)

    def block(h, r, core):
        return msg.at[pl.ds(16 * h + 4 * r + 2 * core, 2)]

    def to_partner_y(r):
        return remote(block(yo, r, co), part_y.at[r], s_py.at[r], r_py.at[r], partner)

    def to_partner_o(r):
        return remote(block(y, r, co), part_o.at[r], s_po.at[r], r_po.at[r], partner)

    def to_across(r):
        return remote(send_y.at[r], recv_y.at[r], s_y.at[r], r_y.at[r], across)

    def ctx_copy(r):
        return remote(ctx_s.at[r], ctx_r.at[r], s_c.at[r], r_c.at[r], partner)

    for r in range(RCH):
        to_partner_y(r).start()
    for r in range(RCH):
        to_partner_o(r).start()
    for q in range(QCH):
        w_copy(q).start()
    x_copy.start()

    def put(dst, k, acc, top, total):
        dst[k, :96, :] = acc
        row = lax.broadcasted_iota(jnp.int32, (8, 128), 0)
        dst[k, 96:104, :] = jnp.where(row == 0, top, total)

    def other_rows(r, carry):
        to_partner_y(r).wait_recv()
        for k in range(2):
            acc, top, total, _ = scaled_sum(msg[16 * yo + 4 * r + 2 * c + k], part_y[r, k])
            put(send_y.at[r], k, acc, top, total)
        to_across(r).start()
        return carry

    lax.fori_loop(0, RCH, other_rows, 0)

    def own_rows(r, carry):
        to_partner_o(r).wait_recv()
        for k in range(2):
            acc, top, total, _ = scaled_sum(msg[16 * y + 4 * r + 2 * c + k], part_o[r, k])
            put(comb_o.at[r], k, acc, top, total)
        return carry

    lax.fori_loop(0, RCH, own_rows, 0)

    def context(r):
        to_across(r).wait_recv()
        for k in range(2):
            acc, _, _, total = scaled_sum(comb_o[r, k], recv_y[r, k])
            ctx_t[...] = acc / total
            for h in range(12):
                ctx_s[r, k * 8:(k + 1) * 8, h * 128:(h + 1) * 128] = ctx_t[pl.ds(h, 8, stride=12), :]
        ctx_copy(r).start()

    context(0)
    x_copy.wait()
    for q in range(QCH):
        w_copy(q).wait()

    def rs(j):
        return remote(rs_out.at[j], rs_in.at[j], s_rs.at[j], r_rs.at[j], ahead)

    def ag(j):
        f = fin.at[y, c, j]
        return remote(f, f, s_ag.at[j], r_ag.at[j], behind)

    def fy(j):
        f = fin.at[y, c, j]
        return remote(f, f, s_fy.at[j], r_fy.at[j], across)

    def fy_in(j):
        f = fin.at[yo, c, j]
        return remote(f, f, s_fy.at[j], r_fy.at[j], across)

    def fd(j):
        f = fin.at[y, c, j]
        return remote(f, f, s_fd.at[j], r_fd.at[j], partner)

    def fd_in(j):
        f = fin.at[y, co, j]
        return remote(f, f, s_fd.at[j], r_fd.at[j], partner)

    def fe(j):
        f = fin.at[yo, c, j]
        return remote(f, f, s_fe.at[j], r_fe.at[j], partner)

    def fe_in(j):
        f = fin.at[yo, co, j]
        return remote(f, f, s_fe.at[j], r_fe.at[j], partner)

    lag = 4 * (3 - u)
    lag_y = lag + 4

    def tick(t, carry):
        @pl.when(t < NMSG)
        def _():
            r, q = t // QCH, t % QCH

            @pl.when(q == 0)
            def _():
                ctx_copy(r).wait_recv()
                lhs[c] = ctx_s[r].astype(BF16)
                lhs[co] = ctx_r[r].astype(BF16)

            prod[...] = jnp.dot(lhs[...].reshape(32, lhs.shape[2]), wbuf[q], preferred_element_type=F32)

            @pl.when(u == 0)
            def _():
                rs_out[t] = prod[...]
                rs(t).start()

            @pl.when((u > 0) & (u < 3))
            def _():
                rs(t).wait_recv()
                rs_out[t] = rs_in[t] + prod[...]
                rs(t).start()

            @pl.when(u == 3)
            def _():
                rs(t).wait_recv()
                x = xbuf[pl.ds(pl.multiple_of(r * 32, 32), 32), pl.ds(pl.multiple_of(q * width, width), width)]
                fin[y, c, t] = rs_in[t] + prod[...] + x.astype(F32)
                ag(t).start()
                fy(t).start()
                fd(t).start()

            @pl.when((q == 1) & (r < RCH - 1))
            def _():
                context(r + 1)

        ta = t - lag

        @pl.when((u < 3) & (ta >= 0) & (ta < NMSG))
        def _():
            ag(ta).wait_recv()

            @pl.when(u > 0)
            def _():
                ag(ta).start()

            fy(ta).start()
            fd(ta).start()

        ty = t - lag_y

        @pl.when((ty >= 0) & (ty < NMSG))
        def _():
            fy_in(ty).wait_recv()
            fe(ty).start()

        return carry

    lax.fori_loop(0, NMSG + lag_y, tick, 0)

    def out_copy(h, r):
        at = pl.ds(h * 128 + r * 32, 32)
        return pltpu.make_async_copy(obuf.at[at], out_hbm.at[at], s_out.at[h, r])

    def convert(j, carry):
        r, q = j // QCH, j % QCH
        fd_in(j).wait_recv()
        fe_in(j).wait_recv()
        for h in range(2):
            at = pl.ds(pl.multiple_of(h * 128 + r * 32, 32), 32)
            for k in range(2):
                obuf[at, pl.ds(pl.multiple_of(k * half + q * width, width), width)] = fin[h, k, j].astype(BF16)

        @pl.when(q == QCH - 1)
        def _():
            out_copy(0, r).start()
            out_copy(1, r).start()

        return carry

    lax.fori_loop(0, NMSG, convert, 0)

    def drain(j, carry):
        @pl.when(u < 3)
        def _():
            rs(j).wait_send()

        @pl.when(u > 0)
        def _():
            ag(j).wait_send()

        fy(j).wait_send()
        fd(j).wait_send()
        fe(j).wait_send()
        return carry

    lax.fori_loop(0, NMSG, drain, 0)
    for r in range(RCH):
        to_partner_y(r).wait_send()
        to_partner_o(r).wait_send()
        to_across(r).wait_send()
        ctx_copy(r).wait_send()
        out_copy(0, r).wait()
        out_copy(1, r).wait()


def finish(msg, hidden, w_o):
    rows, width = hidden.shape
    depth = w_o.shape[0]
    half = width // 2
    cols = half // QCH
    dma = pltpu.SemaphoreType.DMA
    part = pltpu.VMEM((RCH, 2, 104, 128), F32)
    return pl.pallas_call(
        finish_kernel,
        out_shape=jax.ShapeDtypeStruct((rows, width), BF16),
        in_specs=[VMEM, ANY, ANY],
        out_specs=ANY,
        scratch_shapes=[part, part, part, part, part,
                        pltpu.VMEM((96, 128), F32),
                        pltpu.VMEM((RCH, 16, depth), F32), pltpu.VMEM((RCH, 16, depth), F32),
                        pltpu.VMEM((2, 16, depth), BF16),
                        pltpu.VMEM((QCH, depth, cols), BF16),
                        pltpu.VMEM((rows // 2, half), BF16),
                        pltpu.VMEM((32, cols), F32),
                        pltpu.VMEM((NMSG, 32, cols), F32), pltpu.VMEM((NMSG, 32, cols), F32),
                        pltpu.VMEM((2, 2, NMSG, 32, cols), F32),
                        pltpu.VMEM((rows, width), BF16),
                        dma((RCH,)), dma((RCH,)), dma((RCH,)), dma((RCH,)), dma((RCH,)), dma((RCH,)),
                        dma((RCH,)), dma((RCH,)), dma((QCH,)), dma,
                        dma((NMSG,)), dma((NMSG,)), dma((NMSG,)), dma((NMSG,)), dma((NMSG,)), dma((NMSG,)),
                        dma((NMSG,)), dma((NMSG,)), dma((NMSG,)), dma((NMSG,)), dma((2, RCH))],
        compiler_params=pltpu.CompilerParams(collective_id=0, has_side_effects=True, vmem_limit_bytes=VMEM_LIMIT),
        name="finish",
    )(msg, hidden, w_o)


def solution(mesh):
    def local_step(hidden, ln_gain, ln_bias, w_q, w_k, w_v, w_o, k_cache, v_cache, lengths):
        batch, _, kv, head = k_cache.shape
        freq = 10000.0 ** (-2.0 * np.arange(32, dtype=np.float32) / np.float32(64))
        freq = np.concatenate([freq, freq, np.zeros(64)]).astype(np.float32)
        angle = lengths.astype(F32)[:, None] * freq
        q, k_new, v_new = qkv(hidden, ln_gain, ln_bias, jnp.cos(angle), jnp.sin(angle), w_q, w_k, w_v)
        msg = attend(lengths, q, k_new, v_new, k_cache, v_cache)
        out = finish(msg, hidden, w_o)
        return out, k_new.reshape(batch, kv, head), v_new.reshape(batch, kv, head)

    row_spec = P('dp', None)
    cache_spec = P('dp', 'sp', 'tp', None)
    head_spec = P('dp', 'tp', None)
    return jax.shard_map(local_step, mesh=mesh, in_specs=(row_spec, P(None), P(None), P(None, 'tp'), P(None, 'tp'), P(None, 'tp'), P('tp', None), cache_spec, cache_spec, P('dp')), out_specs=(row_spec, head_spec, head_spec), check_vma=False)
```

time: 402 us -> 193 us (0.48)
  waiting for transfers between devices: 270 us -> 0 us
  Pallas kernels: 0 us -> 183 us
  matrix products: 53 us -> 0 us
  other arithmetic: 32.5 us -> 2.56 us
  local copies, waits for them, and re-layouts: 31.4 us -> 6.52 us
  between operations: 14.4 us -> 0.65 us
    psum x1 -> x0, waiting for transfers between devices: 219 us -> none  [local_step(): summed = lax.psum(partial_out, 'tp')]
    pallas_call x0 -> x3, Pallas kernels: none -> 183 us  [the longest x1 90.9 us: finish(): pl.pallas_call(finish_kernel, out_shape=jax.ShapeDtypeStruct((rows, width...]
    dot_general x7 -> x0, matrix products: 53 us -> none  [the longest x1 13.5 us: local_step(): partial_out = jnp.dot(context, w_o, preferred_element_type=jnp.float32)]
    all_gather x1 -> x0, waiting for transfers between devices: 50.7 us -> none  [local_step(): gathered = lax.all_gather(packed, 'sp', axis=0)]
    reduce_sum x5 -> x0, other arithmetic: 13.1 us -> none  [the longest x1 8.08 us: local_step(): jnp.sum(gathered[..., :head_dim] * factor[..., None], axis=0)]
    all_gather x1 -> x0, local copies, waits for them, and re-layouts: 9.79 us -> none  [local_step(): gathered = lax.all_gather(packed, 'sp', axis=0)]
    unnamed x35 -> x1, local copies, waits for them, and re-layouts: 13.3 us -> 3.88 us
    convert_element_type x5 -> x1, other arithmetic: 9.54 us -> 0.68 us  [local_step(): angle = lengths.astype(F32)[:, None] * freq]
  transfers between devices with their start and end apart: 2 -> 0, of which waited for: 2 -> 0; matrix products, arithmetic and copies ran while one was open for 1% -> 0% of each run, Pallas kernels for 0% -> 0%
where the time goes in v1:
time: 193 us
  Pallas kernels  183 us (95%)
  local copies, waits for them, and re-layouts  6.52 us (3%)
  other arithmetic  2.56 us (1%)
    pallas_call x1, Pallas kernels, finish(): pl.pallas_call(finish_kernel, out_shape=jax.ShapeDtypeStruct((rows, width...  90.9 us
    pallas_call x1, Pallas kernels, attend(): pl.pallas_call(functools.partial(attend_kernel, positions=positions, scal...  66.1 us
    pallas_call x1, Pallas kernels, qkv(): pl.pallas_call(qkv_kernel, out_shape=(jax.ShapeDtypeStruct((rows * 16, 12...  26.3 us
    unnamed x1, local copies, waits for them, and re-layouts  3.88 us

profile of v1, /device:TPU:0, one launch (start us, length us, event | category | flops | bytes accessed | tf_op | source)
XLA Modules:
  0.0 193.1 jit_solution(9765341790061641760)
XLA Ops:
  0.6 0.7 convert_element_type.3
  1.3 1.3 reshape.26.gain_ref
  2.6 1.3 reshape.27.bias_ref
  4.0 1.9 multiply_sine_fusion
  5.8 26.3 %qkv.1 = (bf16[4096,128]{1,0:T(8,128)(2,1)}, bf16[512,128]{1,0:T(8,128)(2,1)}, bf16[512,128]{1,0:T(8,128)(2,1)}) custom-call(bf16[1,6144]{1,0:T(2,128)(2,1)} %reshape.26.gain_ref, bf16[1,6144]{1,0:T(2,128)(2,1)} %reshape.27.bias_ref, f32[256,128]{1,0:T(8,128)} %get-tuple-element.10.cos_ref, f32[256,128]{1,0:T(8,128)} %get-tuple-element.9.sin_ref, ...), custom_call_target="tpu_custom_call" | custom-call | tf_op jit(solution)/shard_map/qkv/pallas_call | solution.py:87
  32.2 66.1 %attend.1.msg = f32[32,104,128]{2,1,0:T(8,128)} custom-call(s32[256]{0:T(256)} %len_ref.1, bf16[4096,128]{1,0:T(8,128)(2,1)} %get-tuple-element.6.q_ref, bf16[512,128]{1,0:T(8,128)(2,1)} %get-tuple-element.7.kn_ref, bf16[512,128]{1,0:T(8,128)(2,1)} %get-tuple-element.8.vn_ref, bf16[256,256,128]{2,1,0:T(8,128)(2,1)} %bitcast.4, bf16[256,256,128]{2,1,0:T(8,128)(2,1)} %bitcast.5), custom_call_target="tpu_custom_call" | custom-call | tf_op jit(solution)/shard_map/attend/pallas_call | solution.py:149
  98.3 90.9 %finish.1 = bf16[256,6144]{1,0:T(8,128)(2,1)} custom-call(f32[32,104,128]{2,1,0:T(8,128)} %attend.1.msg, bf16[256,6144]{1,0:T(8,128)(2,1)} %x_hbm.3, bf16[1536,6144]{1,0:T(8,128)(2,1)} %w_hbm.1), custom_call_target="tpu_custom_call" | custom-call | tf_op jit(solution)/shard_map/finish/pallas_call | solution.py:428
  189.2 3.9 %copy.15 = bf16[256,6144]{1,0:T(8,128)(2,1)} copy(bf16[256,6144]{1,0:T(8,128)(2,1)} %finish.1) | data formatting | bytes 6291456

commit v2 on v1

--- a/solution.py
+++ b/solution.py
@@ -17,12 +17,14 @@
 VMEM = pl.BlockSpec(memory_space=pltpu.VMEM)
 
 
-def qkv_kernel(gain_ref, bias_ref, cos_ref, sin_ref, x_hbm, wq_hbm, wk_hbm, wv_hbm,
-               q_out, k_out, v_out, xbuf, hbuf, wbuf, qf, kf, xsem, wsem):
+def qkv_kernel(len_ref, freq_ref, gain_ref, bias_ref, x_hbm, wq_hbm, wk_hbm, wv_hbm,
+               q_out, k_out, v_out, xbuf, hbuf, wbuf, pbuf, qf, kf, cosb, sinb, gainb, biasb, xsem, wsem):
     rows, width = xbuf.shape
     n_q = wq_hbm.shape[1] // 256
-
-    pltpu.make_async_copy(x_hbm, xbuf, xsem).start()
+    tiles = width // 128
+
+    x_copy = pltpu.make_async_copy(x_hbm, xbuf, xsem)
+    x_copy.start()
 
     def q_copy(i):
         return pltpu.make_async_copy(wq_hbm.at[:, pl.ds(i * 256, 256)], wbuf.at[i], wsem.at[i])
@@ -34,56 +36,80 @@
     k_copy.start()
     v_copy.start()
 
-    qf[...] = jnp.zeros_like(qf)
-    pltpu.make_async_copy(x_hbm, xbuf, xsem).wait()
-    gain = 1.0 + gain_ref[...].astype(F32)
-    bias = bias_ref[...].astype(F32)
+    for k in range(tiles):
+        gainb[:, k * 128:(k + 1) * 128] = jnp.broadcast_to(1.0 + gain_ref[k:k + 1, :].astype(F32), (8, 128))
+        biasb[:, k * 128:(k + 1) * 128] = jnp.broadcast_to(bias_ref[k:k + 1, :].astype(F32), (8, 128))
+    for i in range(rows // 128):
+        place = jnp.transpose(jnp.broadcast_to(len_ref[i:i + 1, :].astype(F32), (128, 128)))
+        angle = place * freq_ref[...]
+        cosb[i * 128:(i + 1) * 128, :] = jnp.cos(angle)
+        sinb[i * 128:(i + 1) * 128, :] = jnp.sin(angle)
+
+    x_copy.wait()
 
     def norm(i, carry):
-        at = pl.ds(pl.multiple_of(i * 16, 16), 16)
-        wide = xbuf[at, :].astype(F32)
-        mean = jnp.sum(wide, axis=-1, keepdims=True) * (1.0 / width)
-        centred = wide - mean
-        var = jnp.sum(centred * centred, axis=-1, keepdims=True) * (1.0 / width)
-        hbuf[at, :] = (centred * lax.rsqrt(var + 1e-5) * gain + bias).astype(BF16)
-        return carry
-
-    lax.fori_loop(0, rows // 16, norm, 0)
+        ats = [pl.ds(pl.multiple_of(i * 64 + j * 16, 16), 16) for j in range(4)]
+        lanes = [slice(k * 128, (k + 1) * 128) for k in range(tiles)]
+        means, scales = [], []
+        for at in ats:
+            accs = [xbuf[at, lanes[k]].astype(F32) for k in range(2)]
+            for k in range(2, tiles):
+                accs[k % 2] = accs[k % 2] + xbuf[at, lanes[k]].astype(F32)
+            mean = jnp.sum(accs[0] + accs[1], axis=-1, keepdims=True) * (1.0 / width)
+            means.append(jnp.broadcast_to(mean, (16, 128)))
+        for at, mean in zip(ats, means):
+            accs = [jnp.zeros((16, 128), F32) for _ in range(2)]
+            for k in range(tiles):
+                centred = xbuf[at, lanes[k]].astype(F32) - mean
+                accs[k % 2] = accs[k % 2] + centred * centred
+            var = jnp.sum(accs[0] + accs[1], axis=-1, keepdims=True) * (1.0 / width)
+            scales.append(jnp.broadcast_to(lax.rsqrt(var + 1e-5), (16, 128)))
+        for k in range(tiles):
+            gain = jnp.concatenate([gainb[:, lanes[k]]] * 2, axis=0)
+            bias = jnp.concatenate([biasb[:, lanes[k]]] * 2, axis=0)
+            for at, mean, scale in zip(ats, means, scales):
+                hbuf[at, lanes[k]] = ((xbuf[at, lanes[k]].astype(F32) - mean) * scale * gain + bias).astype(BF16)
+        return carry
+
+    lax.fori_loop(0, rows // 64, norm, 0)
 
     lane = lax.broadcasted_iota(jnp.int32, (rows, 128), 1)
 
     def rotate(u):
         other = jnp.where(lane < 32, -pltpu.roll(u, 96, 1), pltpu.roll(u, 32, 1))
-        turned = u * cos_ref[...] + other * sin_ref[...]
+        turned = u * cosb[...] + other * sinb[...]
         return jnp.where(lane < 64, turned, u)
 
     def project(i):
         return jnp.dot(hbuf[...], wbuf[i], preferred_element_type=F32)
 
-    def q_tile(i, carry):
-        q_copy(i).wait()
-        prod = project(i)
+    def place_heads(i, prod):
         for head in range(2):
-            qf[pl.ds(2 * i + head, rows, stride=16), :] = rotate(prod[:, head * 128:(head + 1) * 128])
-        return carry
-
-    lax.fori_loop(0, n_q, q_tile, 0)
-    k_copy.wait()
-    prod = project(n_q)
-    for head in range(2):
-        kf[pl.ds(head, rows, stride=2), :] = rotate(prod[:, head * 128:(head + 1) * 128])
-    k_out[...] = kf[...].astype(BF16)
-    v_copy.wait()
-    prod = project(n_q + 1)
-    for head in range(2):
-        kf[pl.ds(head, rows, stride=2), :] = prod[:, head * 128:(head + 1) * 128]
-    v_out[...] = kf[...].astype(BF16)
+            u = prod[:, head * 128:(head + 1) * 128]
+            qf[pl.ds(lax.rem(2 * i + head, 16), rows, stride=16), :] = jnp.where(i == n_q + 1, u, rotate(u))
+
+    pbuf[1] = jnp.zeros((rows, 256), F32)
+
+    def tile(i, carry):
+        pltpu.make_async_copy(wk_hbm, wbuf.at[i], wsem.at[i]).wait()
+        pbuf[lax.rem(i, 2)] = project(i)
+        place_heads(i + n_q + 1, pbuf[lax.rem(i + 1, 2)])
+        return carry
+
+    lax.fori_loop(0, n_q + 2, tile, 0)
+    place_heads(n_q + 1, pbuf[(n_q + 1) % 2])
+    for ref, row in ((k_out, 12), (v_out, 14)):
+        for head in range(2):
+            kf[pl.ds(head, rows, stride=2), :] = qf[pl.ds(row + head, rows, stride=16), :]
+        ref[...] = kf[...].astype(BF16)
     q_out[...] = qf[...].astype(BF16)
 
 
-def qkv(hidden, gain, bias, cos, sin, w_q, w_k, w_v):
+def qkv(hidden, gain, bias, lengths, w_q, w_k, w_v):
     rows, width = hidden.shape
     n_tiles = w_q.shape[1] // 256 + 2
+    freq = 10000.0 ** (-2.0 * np.arange(32, dtype=np.float32) / np.float32(64))
+    freq = np.concatenate([freq, freq, np.zeros(64)]).astype(np.float32).reshape(1, 128)
     return pl.pallas_call(
         qkv_kernel,
         out_shape=(jax.ShapeDtypeStruct((rows * 16, 128), BF16),
@@ -92,72 +118,95 @@
         in_specs=[VMEM, VMEM, VMEM, VMEM, ANY, ANY, ANY, ANY],
         out_specs=(VMEM, VMEM, VMEM),
         scratch_shapes=[pltpu.VMEM((rows, width), BF16), pltpu.VMEM((rows, width), BF16),
-                        pltpu.VMEM((n_tiles, width, 256), BF16),
+                        pltpu.VMEM((n_tiles, width, 256), BF16), pltpu.VMEM((2, rows, 256), F32),
                         pltpu.VMEM((rows * 16, 128), F32), pltpu.VMEM((rows * 2, 128), F32),
+                        pltpu.VMEM((rows, 128), F32), pltpu.VMEM((rows, 128), F32),
+                        pltpu.VMEM((8, width), F32), pltpu.VMEM((8, width), F32),
                         pltpu.SemaphoreType.DMA, pltpu.SemaphoreType.DMA((n_tiles,))],
         compiler_params=pltpu.CompilerParams(vmem_limit_bytes=VMEM_LIMIT),
         name="qkv",
-    )(gain.reshape(1, width), bias.reshape(1, width), cos, sin, hidden, w_q, w_k, w_v)
-
-
-def attend_kernel(len_ref, q_ref, kn_ref, vn_ref, k_ref, v_ref, o_ref, stat, *, positions, scale):
+    )(lengths.reshape(rows // 128, 128), jnp.asarray(freq), gain.reshape(width // 128, 128),
+      bias.reshape(width // 128, 128), hidden, w_q, w_k, w_v)
+
+
+STEP8 = 4
+
+
+def attend_kernel(len_ref, q_ref, kn_ref, vn_ref, k_ref, v_ref, o_ref, sbuf, self_buf, wbuf, stat, *, positions, scale):
     step = pl.program_id(0)
     first = lax.axis_index("sp") * positions
     col = lax.broadcasted_iota(jnp.int32, (16, 2 * positions), 1)
     row = lax.broadcasted_iota(jnp.int32, (16, 2 * positions), 0)
     group = jnp.where(row >= 6, 1, 0)
     place = jnp.where(lax.rem(col, 2) == group, first + col // 2, 1 << 30)
-    row16 = lax.broadcasted_iota(jnp.int32, (16, 16), 0)
-    col16 = lax.broadcasted_iota(jnp.int32, (16, 16), 1)
-    group16 = jnp.where(row16 >= 6, 1, 0)
-    lane = lax.broadcasted_iota(jnp.int32, (16, 128), 1)
     pick_row = lax.broadcasted_iota(jnp.int32, (128, 16), 0)
     pick_col = lax.broadcasted_iota(jnp.int32, (128, 16), 1)
     pick = pick_col == 2 * (pick_row // 16) + jnp.where(lax.rem(pick_row, 16) >= 6, 1, 0)
-    pick = jnp.where(pick, 1.0, 0.0).astype(BF16)
+    spread = jnp.where(pick, 1.0, 0.0).astype(BF16)
+    lane = lax.broadcasted_iota(jnp.int32, (128, 128), 1)
     nt = (((1,), (1,)), ((), ()))
-    stat[...] = jnp.zeros_like(stat)
-    for half in range(2):
-        q8 = q_ref[half * 128:(half + 1) * 128, :]
-        self8 = lax.dot_general(q8, kn_ref[half * 16:(half + 1) * 16, :], nt, preferred_element_type=F32) * scale
-        v8 = jnp.dot(pick, vn_ref[half * 16:(half + 1) * 16, :], preferred_element_type=F32)
+    own_w = [None] * STEP8
+
+    def scores(g):
+        q8 = q_ref[g * 128:(g + 1) * 128, :]
+        self8 = lax.dot_general(q8, kn_ref[g * 16:(g + 1) * 16, :], nt, preferred_element_type=F32) * scale
+        self8 = jnp.where(pick, self8, NEG)
         for b in range(8):
-            length = len_ref[step * 16 + half * 8 + b]
+            at = slice(g * 128 + b * 16, g * 128 + (b + 1) * 16)
+            length = len_ref[(step * STEP8 + g) * 8 + b]
             owner = (length >= first) & (length < first + positions)
-            s = lax.dot_general(q8[b * 16:(b + 1) * 16, :], k_ref[half * 8 + b], nt, preferred_element_type=F32) * scale
-            s = jnp.where(place < length, s, NEG)
-            mine = jnp.where(col16 == 2 * b + group16, self8[b * 16:(b + 1) * 16, :], NEG)
-            own = jnp.max(mine, axis=1, keepdims=True)
-            own = jnp.where(owner, own, NEG)
-            top = jnp.maximum(jnp.max(s, axis=1, keepdims=True), own)
-            w = jnp.exp(s - top)
-            w_own = jnp.exp(own - top)
-            total = jnp.sum(w, axis=1, keepdims=True) + w_own
-            acc = jnp.dot(w.astype(BF16), v_ref[half * 8 + b], preferred_element_type=F32)
-            acc = acc + w_own * v8[b * 16:(b + 1) * 16, :]
-            o_ref[half, b * 12:(b + 1) * 12, :] = acc[:12, :]
-            pair = jnp.where(lane == 0, top, total)
-            stat[half, b * 12:(b + 1) * 12, :] = pair[:12, :]
-        o_ref[half, 96:104, :] = jnp.transpose(stat[half])[:8, :]
+            s = lax.dot_general(q_ref[at, :], k_ref[g * 8 + b], nt, preferred_element_type=F32) * scale
+            sbuf[at, :] = jnp.where(place < length, s, NEG)
+            self_buf[at, :] = jnp.where(owner, self8[b * 16:(b + 1) * 16, :], NEG)
+
+    def weights(g):
+        at = slice(g * 128, (g + 1) * 128)
+        s = sbuf[at, :]
+        own = jnp.max(self_buf[at, :], axis=1, keepdims=True)
+        top = jnp.maximum(jnp.max(s, axis=1, keepdims=True), own)
+        w = jnp.exp(s - top)
+        own_w[g] = jnp.exp(own - top)
+        total = jnp.sum(w, axis=1, keepdims=True) + own_w[g]
+        wbuf[at, :] = w.astype(BF16)
+        stat[at, :] = jnp.where(lane == 0, top, total)
+
+    def sums(g):
+        v8 = jnp.dot(spread, vn_ref[g * 16:(g + 1) * 16, :], preferred_element_type=F32)
+        own8 = own_w[g] * v8
+        turned = jnp.transpose(stat[g * 128:(g + 1) * 128, :])[:8, :]
+        o_ref[g, 96:104, :] = jnp.concatenate([turned[:, b * 16:b * 16 + 12] for b in range(8)] + [jnp.zeros((8, 32), F32)], axis=1)
+        for b in range(8):
+            at = slice(g * 128 + b * 16, g * 128 + (b + 1) * 16)
+            acc = jnp.dot(wbuf[at, :], v_ref[g * 8 + b], preferred_element_type=F32) + own8[b * 16:(b + 1) * 16, :]
+            o_ref[g, b * 12:(b + 1) * 12, :] = acc[:12, :]
+
+    for g in range(STEP8 + 2):
+        if g < STEP8:
+            scores(g)
+        if 1 <= g <= STEP8:
+            weights(g - 1)
+        if g >= 2:
+            sums(g - 2)
 
 
 def attend(lengths, q, k_new, v_new, k_cache, v_cache):
     batch, positions, kv, head = k_cache.shape
     k_rows = k_cache.reshape(batch, positions * kv, head)
     v_rows = v_cache.reshape(batch, positions * kv, head)
-    steps = batch // 16
+    take = STEP8 * 8
     return pl.pallas_call(
         functools.partial(attend_kernel, positions=positions, scale=head ** -0.5),
         out_shape=jax.ShapeDtypeStruct((batch // 8, 104, 128), F32),
         grid_spec=pltpu.PrefetchScalarGridSpec(
-            num_scalar_prefetch=1, grid=(steps,),
-            in_specs=[pl.BlockSpec((256, 128), lambda i, n: (i, 0)),
-                      pl.BlockSpec((32, 128), lambda i, n: (i, 0)),
-                      pl.BlockSpec((32, 128), lambda i, n: (i, 0)),
-                      pl.BlockSpec((16, positions * kv, head), lambda i, n: (i, 0, 0)),
-                      pl.BlockSpec((16, positions * kv, head), lambda i, n: (i, 0, 0))],
-            out_specs=pl.BlockSpec((2, 104, 128), lambda i, n: (i, 0, 0)),
-            scratch_shapes=[pltpu.VMEM((2, 128, 128), F32)]),
+            num_scalar_prefetch=1, grid=(batch // take,),
+            in_specs=[pl.BlockSpec((take * 16, 128), lambda i, n: (i, 0)),
+                      pl.BlockSpec((take * 2, 128), lambda i, n: (i, 0)),
+                      pl.BlockSpec((take * 2, 128), lambda i, n: (i, 0)),
+                      pl.BlockSpec((take, positions * kv, head), lambda i, n: (i, 0, 0)),
+                      pl.BlockSpec((take, positions * kv, head), lambda i, n: (i, 0, 0))],
+            out_specs=pl.BlockSpec((STEP8, 104, 128), lambda i, n: (i, 0, 0)),
+            scratch_shapes=[pltpu.VMEM((take * 16, positions * kv), F32), pltpu.VMEM((take * 16, 16), F32),
+                            pltpu.VMEM((take * 16, positions * kv), BF16), pltpu.VMEM((take * 16, 128), F32)]),
         compiler_params=pltpu.CompilerParams(vmem_limit_bytes=VMEM_LIMIT),
         name="attend",
     )(lengths, q, k_new, v_new, k_rows, v_rows)
@@ -452,10 +501,7 @@
 def solution(mesh):
     def local_step(hidden, ln_gain, ln_bias, w_q, w_k, w_v, w_o, k_cache, v_cache, lengths):
         batch, _, kv, head = k_cache.shape
-        freq = 10000.0 ** (-2.0 * np.arange(32, dtype=np.float32) / np.float32(64))
-        freq = np.concatenate([freq, freq, np.zeros(64)]).astype(np.float32)
-        angle = lengths.astype(F32)[:, None] * freq
-        q, k_new, v_new = qkv(hidden, ln_gain, ln_bias, jnp.cos(angle), jnp.sin(angle), w_q, w_k, w_v)
+        q, k_new, v_new = qkv(hidden, ln_gain, ln_bias, lengths, w_q, w_k, w_v)
         msg = attend(lengths, q, k_new, v_new, k_cache, v_cache)
         out = finish(msg, hidden, w_o)
         return out, k_new.reshape(batch, kv, head), v_new.reshape(batch, kv, head)

time: 193 us -> 136 us (0.70)
  Pallas kernels: 183 us -> 132 us
  local copies, waits for them, and re-layouts: 6.52 us -> 3.88 us
  other arithmetic: 2.56 us -> 0 us
    pallas_call x1, Pallas kernels: 66.1 us -> 17.5 us  [attend(): pl.pallas_call(functools.partial(attend_kernel, positions=positions, scal...]
    pallas_call x1, Pallas kernels: 26.3 us -> 23.2 us  [qkv(): pl.pallas_call(qkv_kernel, out_shape=(jax.ShapeDtypeStruct((rows * 16, 12...]
    reshape x2 -> x0, local copies, waits for them, and re-layouts: 2.64 us -> none  [the longest x1 1.32 us: qkv(): gain.reshape(1, width)]
where the time goes in v2:
time: 136 us
  Pallas kernels  132 us (97%)
  local copies, waits for them, and re-layouts  3.88 us (3%)
    pallas_call x1, Pallas kernels, finish(): pl.pallas_call(finish_kernel, out_shape=jax.ShapeDtypeStruct((rows, width...  91 us
    pallas_call x1, Pallas kernels, qkv(): pl.pallas_call(qkv_kernel, out_shape=(jax.ShapeDtypeStruct((rows * 16, 12...  23.2 us
    pallas_call x1, Pallas kernels, attend(): pl.pallas_call(functools.partial(attend_kernel, positions=positions, scal...  17.5 us
    unnamed x1, local copies, waits for them, and re-layouts  3.88 us

profile of v2, /device:TPU:0, one launch (start us, length us, event | category | flops | bytes accessed | tf_op | source)
XLA Modules:
  0.0 136.2 jit_solution(16824392403075249995)
XLA Ops:
  0.6 23.2 %qkv.1 = (bf16[4096,128]{1,0:T(8,128)(2,1)}, bf16[512,128]{1,0:T(8,128)(2,1)}, bf16[512,128]{1,0:T(8,128)(2,1)}) custom-call(s32[2,128]{1,0:T(2,128)} %bitcast.13, f32[1,128]{1,0:T(1,128)} %constant.2.clone.freq_ref, bf16[48,128]{1,0:T(8,128)(2,1)} %bitcast.11, bf16[48,128]{1,0:T(8,128)(2,1)} %bitcast.12, bf16[256,6144]{1,0:T(8,128)(2,1)} %x_hbm.3, ...), custom_call_target="tpu_custom_call" | custom-call | tf_op jit(solution)/shard_map/qkv/pallas_call | solution.py:113
  23.9 17.5 %attend.1.msg = f32[32,104,128]{2,1,0:T(8,128)} custom-call(s32[256]{0:T(256)} %len_ref.1, bf16[4096,128]{1,0:T(8,128)(2,1)} %get-tuple-element.6.q_ref, bf16[512,128]{1,0:T(8,128)(2,1)} %get-tuple-element.7.kn_ref, bf16[512,128]{1,0:T(8,128)(2,1)} %get-tuple-element.8.vn_ref, bf16[256,256,128]{2,1,0:T(8,128)(2,1)} %bitcast.7, bf16[256,256,128]{2,1,0:T(8,128)(2,1)} %bitcast.8), custom_call_target="tpu_custom_call" | custom-call | tf_op jit(solution)/shard_map/attend/pallas_call | solution.py:197
  41.3 91.0 %finish.1 = bf16[256,6144]{1,0:T(8,128)(2,1)} custom-call(f32[32,104,128]{2,1,0:T(8,128)} %attend.1.msg, bf16[256,6144]{1,0:T(8,128)(2,1)} %x_hbm.3, bf16[1536,6144]{1,0:T(8,128)(2,1)} %w_hbm.1), custom_call_target="tpu_custom_call" | custom-call | tf_op jit(solution)/shard_map/finish/pallas_call | solution.py:477
  132.3 3.9 %copy.15 = bf16[256,6144]{1,0:T(8,128)(2,1)} copy(bf16[256,6144]{1,0:T(8,128)(2,1)} %finish.1) | data formatting | bytes 6291456

commit v3 on v2

v3 whole, which is shorter than its diff:
```python
import functools

import jax
import jax.numpy as jnp
import numpy as np
from jax import lax
from jax.experimental import pallas as pl
from jax.experimental.pallas import tpu as pltpu
from jax.sharding import PartitionSpec as P

F32 = jnp.float32
BF16 = jnp.bfloat16
MESH = pl.DeviceIdType.MESH
NEG = -0.7 * float(np.finfo(np.float32).max)
VMEM_LIMIT = 60 * 1024 * 1024
ANY = pl.BlockSpec(memory_space=pl.ANY)
VMEM = pl.BlockSpec(memory_space=pltpu.VMEM)


def qkv_kernel(len_ref, freq_ref, gain_ref, bias_ref, x_hbm, wq_hbm, wk_hbm, wv_hbm,
               q_out, k_out, v_out, xbuf, hbuf, wbuf, pbuf, qf, kf, cosb, sinb, gainb, biasb, xsem, wsem):
    rows, width = xbuf.shape
    n_q = wq_hbm.shape[1] // 256
    tiles = width // 128

    x_copy = pltpu.make_async_copy(x_hbm, xbuf, xsem)
    x_copy.start()

    def q_copy(i):
        return pltpu.make_async_copy(wq_hbm.at[:, pl.ds(i * 256, 256)], wbuf.at[i], wsem.at[i])

    k_copy = pltpu.make_async_copy(wk_hbm, wbuf.at[n_q], wsem.at[n_q])
    v_copy = pltpu.make_async_copy(wv_hbm, wbuf.at[n_q + 1], wsem.at[n_q + 1])
    for k in range(tiles):
        gainb[:, k * 128:(k + 1) * 128] = jnp.broadcast_to(1.0 + gain_ref[k:k + 1, :].astype(F32), (8, 128))
        biasb[:, k * 128:(k + 1) * 128] = jnp.broadcast_to(bias_ref[k:k + 1, :].astype(F32), (8, 128))
    for i in range(rows // 128):
        place = jnp.transpose(jnp.broadcast_to(len_ref[i:i + 1, :].astype(F32), (128, 128)))
        angle = place * freq_ref[...]
        cosb[i * 128:(i + 1) * 128, :] = jnp.cos(angle)
        sinb[i * 128:(i + 1) * 128, :] = jnp.sin(angle)

    x_copy.wait()
    q_copy(0).start()
    q_copy(1).start()

    def norm(i, carry):
        @pl.when(i < n_q - 2)
        def _():
            q_copy(i + 2).start()

        ats = [pl.ds(pl.multiple_of(i * 64 + j * 16, 16), 16) for j in range(4)]
        lanes = [slice(k * 128, (k + 1) * 128) for k in range(tiles)]
        means, scales = [], []
        for at in ats:
            accs = [xbuf[at, lanes[k]].astype(F32) for k in range(2)]
            for k in range(2, tiles):
                accs[k % 2] = accs[k % 2] + xbuf[at, lanes[k]].astype(F32)
            mean = jnp.sum(accs[0] + accs[1], axis=-1, keepdims=True) * (1.0 / width)
            means.append(jnp.broadcast_to(mean, (16, 128)))
        for at, mean in zip(ats, means):
            accs = [jnp.zeros((16, 128), F32) for _ in range(2)]
            for k in range(tiles):
                centred = xbuf[at, lanes[k]].astype(F32) - mean
                accs[k % 2] = accs[k % 2] + centred * centred
            var = jnp.sum(accs[0] + accs[1], axis=-1, keepdims=True) * (1.0 / width)
            scales.append(jnp.broadcast_to(lax.rsqrt(var + 1e-5), (16, 128)))
        for k in range(tiles):
            gain = jnp.concatenate([gainb[:, lanes[k]]] * 2, axis=0)
            bias = jnp.concatenate([biasb[:, lanes[k]]] * 2, axis=0)
            for at, mean, scale in zip(ats, means, scales):
                hbuf[at, lanes[k]] = ((xbuf[at, lanes[k]].astype(F32) - mean) * scale * gain + bias).astype(BF16)
        return carry

    lax.fori_loop(0, rows // 64, norm, 0)
    k_copy.start()
    v_copy.start()

    lane = lax.broadcasted_iota(jnp.int32, (rows, 128), 1)

    def rotate(u):
        other = jnp.where(lane < 32, -pltpu.roll(u, 96, 1), pltpu.roll(u, 32, 1))
        turned = u * cosb[...] + other * sinb[...]
        return jnp.where(lane < 64, turned, u)

    def project(i):
        return jnp.dot(hbuf[...], wbuf[i], preferred_element_type=F32)

    def place_heads(i, prod):
        for head in range(2):
            u = prod[:, head * 128:(head + 1) * 128]
            qf[pl.ds(lax.rem(2 * i + head, 16), rows, stride=16), :] = jnp.where(i == n_q + 1, u, rotate(u))

    pbuf[1] = jnp.zeros((rows, 256), F32)

    def tile(i, carry):
        pltpu.make_async_copy(wk_hbm, wbuf.at[i], wsem.at[i]).wait()
        pbuf[lax.rem(i, 2)] = project(i)
        place_heads(i + n_q + 1, pbuf[lax.rem(i + 1, 2)])
        return carry

    lax.fori_loop(0, n_q + 2, tile, 0)
    place_heads(n_q + 1, pbuf[(n_q + 1) % 2])
    for ref, row in ((k_out, 12), (v_out, 14)):
        for head in range(2):
            kf[pl.ds(head, rows, stride=2), :] = qf[pl.ds(row + head, rows, stride=16), :]
        ref[...] = kf[...].astype(BF16)
    q_out[...] = qf[...].astype(BF16)


def qkv(hidden, gain, bias, lengths, w_q, w_k, w_v):
    rows, width = hidden.shape
    n_tiles = w_q.shape[1] // 256 + 2
    freq = 10000.0 ** (-2.0 * np.arange(32, dtype=np.float32) / np.float32(64))
    freq = np.concatenate([freq, freq, np.zeros(64)]).astype(np.float32).reshape(1, 128)
    return pl.pallas_call(
        qkv_kernel,
        out_shape=(jax.ShapeDtypeStruct((rows * 16, 128), BF16),
                   jax.ShapeDtypeStruct((rows * 2, 128), BF16),
                   jax.ShapeDtypeStruct((rows * 2, 128), BF16)),
        in_specs=[VMEM, VMEM, VMEM, VMEM, ANY, ANY, ANY, ANY],
        out_specs=(VMEM, VMEM, VMEM),
        scratch_shapes=[pltpu.VMEM((rows, width), BF16), pltpu.VMEM((rows, width), BF16),
                        pltpu.VMEM((n_tiles, width, 256), BF16), pltpu.VMEM((2, rows, 256), F32),
                        pltpu.VMEM((rows * 16, 128), F32), pltpu.VMEM((rows * 2, 128), F32),
                        pltpu.VMEM((rows, 128), F32), pltpu.VMEM((rows, 128), F32),
                        pltpu.VMEM((8, width), F32), pltpu.VMEM((8, width), F32),
                        pltpu.SemaphoreType.DMA, pltpu.SemaphoreType.DMA((n_tiles,))],
        compiler_params=pltpu.CompilerParams(vmem_limit_bytes=VMEM_LIMIT),
        name="qkv",
    )(lengths.reshape(rows // 128, 128), jnp.asarray(freq), gain.reshape(width // 128, 128),
      bias.reshape(width // 128, 128), hidden, w_q, w_k, w_v)


RCH = 4
QCH = 6
NMSG = RCH * QCH
PER = QCH // 2
STEPS = 2 * RCH
HOP = 3
LAG = 6
SLOTS = 3


def scaled_sum(a, b):
    m_a, l_a, m_b, l_b = a[96:97, :], a[97:98, :], b[96:97, :], b[97:98, :]
    top = jnp.maximum(m_a, m_b)
    f_a, f_b = jnp.exp(m_a - top), jnp.exp(m_b - top)
    total = l_a * f_a + l_b * f_b
    r = lax.broadcasted_iota(jnp.int32, (128, 128), 0)
    turned = jnp.transpose(jnp.where(r == 0, f_a, jnp.where(r == 1, f_b, total)))
    acc = a[:96, :] * turned[:96, 0:1] + b[:96, :] * turned[:96, 1:2]
    return acc, top, total, turned[:96, 2:3]


def block_kernel(len_ref, q_ref, kn_ref, vn_ref, k_hbm, v_hbm, x_hbm, w_hbm, out_hbm,
                 kbuf, vbuf, sbuf, self_buf, pbuf, stat, msg, part, send_y, recv_y, comb_o, ctx_t, ctx_s, ctx_r,
                 lhs, wbuf, xbuf, prod, rs_in, rs_out, fin, obuf,
                 s_k, s_v, s_p, r_p, s_y, r_y, s_c, r_c, s_w, s_x,
                 s_rs, r_rs, s_ag, r_ag, s_fy, r_fy, s_fd, r_fd, s_fe, r_fe, s_out, *, positions, scale):
    d, z, s = lax.axis_index("dp"), lax.axis_index("tp"), lax.axis_index("sp")
    y, c = s // 2, s % 2
    yo, co = 1 - y, 1 - c
    u = c * z + co * (3 - z)
    partner, across = (d, z, 2 * y + co), (d, z, 2 * yo + c)
    ahead, behind = (d, z + 2 * c - 1, s), (d, z - 2 * c + 1, s)
    half = wbuf.shape[0] * wbuf.shape[2]
    width = wbuf.shape[2]

    def remote(src, dst, send, recv, dev):
        return pltpu.make_async_remote_copy(src_ref=src, dst_ref=dst, send_sem=send, recv_sem=recv,
                                            device_id=dev, device_id_type=MESH)

    barrier = pltpu.get_barrier_semaphore()
    pl.semaphore_signal(barrier, inc=1, device_id=partner, device_id_type=MESH)
    pl.semaphore_signal(barrier, inc=1, device_id=across, device_id_type=MESH)

    @pl.when(u < 3)
    def _():
        pl.semaphore_signal(barrier, inc=1, device_id=ahead, device_id_type=MESH)

    @pl.when(u > 0)
    def _():
        pl.semaphore_signal(barrier, inc=1, device_id=behind, device_id_type=MESH)

    def first_row(i):
        return 128 * ((i % 2) * y + (1 - i % 2) * yo) + 32 * (i // 2)

    def k_copy(i):
        return pltpu.make_async_copy(k_hbm.at[pl.ds(first_row(i), 32)], kbuf.at[i % SLOTS], s_k.at[i % SLOTS])

    def v_copy(i):
        return pltpu.make_async_copy(v_hbm.at[pl.ds(first_row(i), 32)], vbuf.at[i % SLOTS], s_v.at[i % SLOTS])

    def w_copy(q):
        return pltpu.make_async_copy(w_hbm.at[:, pl.ds(c * half + q * width, width)], wbuf.at[q], s_w.at[q])

    x_copy = pltpu.make_async_copy(x_hbm.at[pl.ds(y * 128, 128), pl.ds(c * half, half)], xbuf, s_x)

    for i in range(SLOTS):
        k_copy(i).start()
        v_copy(i).start()
    x_copy.start()
    pl.semaphore_wait(barrier, 2 + (z + 2) // 3 + (5 - z) // 3)

    first = s * positions
    col = lax.broadcasted_iota(jnp.int32, (16, 2 * positions), 1)
    row = lax.broadcasted_iota(jnp.int32, (16, 2 * positions), 0)
    place = jnp.where(lax.rem(col, 2) == jnp.where(row >= 6, 1, 0), first + col // 2, 1 << 30)
    pick_row = lax.broadcasted_iota(jnp.int32, (128, 16), 0)
    pick_col = lax.broadcasted_iota(jnp.int32, (128, 16), 1)
    pick = pick_col == 2 * (pick_row // 16) + jnp.where(lax.rem(pick_row, 16) >= 6, 1, 0)
    nt = (((1,), (1,)), ((), ()))

    def attention(i):
        k_copy(i).wait()
        v_copy(i).wait()
        slot = i % SLOTS
        base = first_row(i)
        spread = jnp.where(pick, 1.0, 0.0).astype(BF16)
        lane = lax.broadcasted_iota(jnp.int32, (128, 128), 1)
        begin = lax.broadcasted_iota(jnp.int32, (16, 16), 0) * 0 + first
        own_w = [None] * 4

        def scores(g):
            q8 = q_ref[pl.ds(pl.multiple_of(base * 16 + g * 128, 128), 128), :]
            kn = kn_ref[pl.ds(pl.multiple_of(base * 2 + g * 16, 16), 16), :]
            self8 = lax.dot_general(q8, kn, nt, preferred_element_type=F32) * scale
            self8 = jnp.where(pick, self8, NEG)
            for b in range(8):
                at = slice(g * 128 + b * 16, g * 128 + (b + 1) * 16)
                length = len_ref[base + g * 8 + b]
                owner = (length >= begin) & (length < begin + positions)
                sc = lax.dot_general(q8[b * 16:(b + 1) * 16, :], kbuf[slot, g * 8 + b], nt, preferred_element_type=F32) * scale
                sbuf[at, :] = jnp.where(place < length, sc, NEG)
                self_buf[at, :] = jnp.where(owner, self8[b * 16:(b + 1) * 16, :], NEG)

        def weights(g):
            at = slice(g * 128, (g + 1) * 128)
            sc = sbuf[at, :]
            own = jnp.max(self_buf[at, :], axis=1, keepdims=True)
            top = jnp.maximum(jnp.max(sc, axis=1, keepdims=True), own)
            w = jnp.exp(sc - top)
            own_w[g] = jnp.exp(own - top)
            total = jnp.sum(w, axis=1, keepdims=True) + own_w[g]
            pbuf[at, :] = w.astype(BF16)
            stat[at, :] = jnp.where(lane == 0, top, total)

        def sums(g):
            vn = vn_ref[pl.ds(pl.multiple_of(base * 2 + g * 16, 16), 16), :]
            own8 = own_w[g] * jnp.dot(spread, vn, preferred_element_type=F32)
            turned = jnp.transpose(stat[g * 128:(g + 1) * 128, :])[:8, :]
            msg[i, g, 96:104, :] = jnp.concatenate([turned[:, b * 16:b * 16 + 12] for b in range(8)] + [jnp.zeros((8, 32), F32)], axis=1)
            for b in range(8):
                at = slice(g * 128 + b * 16, g * 128 + (b + 1) * 16)
                acc = jnp.dot(pbuf[at, :], vbuf[slot, g * 8 + b], preferred_element_type=F32) + own8[b * 16:(b + 1) * 16, :]
                msg[i, g, b * 12:(b + 1) * 12, :] = acc[:12, :]

        for g in range(6):
            if g < 4:
                scores(g)
            if 1 <= g <= 4:
                weights(g - 1)
            if g >= 2:
                sums(g - 2)

    def to_partner(i):
        return remote(msg.at[i, pl.ds(2 * co, 2)], part.at[i], s_p.at[i], r_p.at[i], partner)

    def to_across(r):
        return remote(send_y.at[r], recv_y.at[r], s_y.at[r], r_y.at[r], across)

    def ctx_copy(r):
        return remote(ctx_s.at[r], ctx_r.at[r], s_c.at[r], r_c.at[r], partner)

    def merge(i, dst):
        to_partner(i).wait_recv()
        for k in range(2):
            acc, top, total, _ = scaled_sum(msg[i, 2 * c + k], part[i, k])
            dst[k, :96, :] = acc
            line = lax.broadcasted_iota(jnp.int32, (8, 128), 0)
            dst[k, 96:104, :] = jnp.where(line == 0, top, total)

    def context(r):
        to_across(r).wait_recv()
        for k in range(2):
            acc, _, _, total = scaled_sum(comb_o[r, k], recv_y[r, k])
            ctx_t[...] = acc / total
            for h in range(12):
                ctx_s[r, k * 8:(k + 1) * 8, h * 128:(h + 1) * 128] = ctx_t[pl.ds(h, 8, stride=12), :]
        ctx_copy(r).start()

    def rs(j):
        return remote(rs_out.at[j], rs_in.at[j], s_rs.at[j], r_rs.at[j], ahead)

    def final(dst, send, recv, h, core, j):
        f = fin.at[h, core, j]
        return remote(f, f, send.at[j], recv.at[j], dst)

    def ag(j):
        return final(behind, s_ag, r_ag, y, c, j)

    def fy(j):
        return final(across, s_fy, r_fy, y, c, j)

    def fy_in(j):
        return final(across, s_fy, r_fy, yo, c, j)

    def fd(j):
        return final(partner, s_fd, r_fd, y, c, j)

    def fd_in(j):
        return final(partner, s_fd, r_fd, y, co, j)

    def fe(j):
        return final(partner, s_fe, r_fe, yo, c, j)

    def fe_in(j):
        return final(partner, s_fe, r_fe, yo, co, j)

    def convert(h, core, j):
        at = pl.ds(pl.multiple_of(h * 128 + (j // QCH) * 32, 32), 32)
        obuf[at, pl.ds(pl.multiple_of(core * half + (j % QCH) * width, width), width)] = fin[h, core, j].astype(BF16)

    lag = LAG * (3 - u)
    lag_y = lag + LAG
    start = 2 * QCH + HOP * u

    def tick(t, carry):
        i, r6 = t // PER, t // QCH

        @pl.when((t < PER * STEPS) & (t % PER == 0))
        def _():
            attention(i)
            to_partner(i).start()

            @pl.when(i < STEPS - SLOTS)
            def _():
                k_copy(i + SLOTS).start()
                v_copy(i + SLOTS).start()

            @pl.when(i < QCH)
            def _():
                w_copy(i).start()

        @pl.when((t % QCH == PER + 1) & (t < NMSG))
        def _():
            merge(2 * r6, send_y.at[r6])
            to_across(r6).start()

        @pl.when((t % QCH == 1) & (t >= QCH) & (t < NMSG + QCH))
        def _():
            merge(2 * r6 - 1, comb_o.at[r6 - 1])

        @pl.when((t % QCH == QCH - 2) & (t >= QCH) & (t < NMSG + QCH))
        def _():
            context(r6 - 1)

        j = t - start

        @pl.when((j >= 0) & (j < NMSG))
        def _():
            r, q = j // QCH, j % QCH

            @pl.when(q == 0)
            def _():
                ctx_copy(r).wait_recv()
                lhs[c] = ctx_s[r].astype(BF16)
                lhs[co] = ctx_r[r].astype(BF16)

            @pl.when(r == 0)
            def _():
                w_copy(q).wait()

            @pl.when(j == 0)
            def _():
                x_copy.wait()

            prod[...] = jnp.dot(lhs[...].reshape(32, lhs.shape[2]), wbuf[q], preferred_element_type=F32)

            @pl.when(u == 0)
            def _():
                rs_out[j] = prod[...]
                rs(j).start()

            @pl.when((u > 0) & (u < 3))
            def _():
                rs(j).wait_recv()
                rs_out[j] = rs_in[j] + prod[...]
                rs(j).start()

            @pl.when(u == 3)
            def _():
                rs(j).wait_recv()
                x = xbuf[pl.ds(pl.multiple_of(r * 32, 32), 32), pl.ds(pl.multiple_of(q * width, width), width)]
                fin[y, c, j] = rs_in[j] + prod[...] + x.astype(F32)
                ag(j).start()
                fy(j).start()
                fd(j).start()
                convert(y, c, j)

        ja = j - lag

        @pl.when((u < 3) & (ja >= 0) & (ja < NMSG))
        def _():
            ag(ja).wait_recv()

            @pl.when(u > 0)
            def _():
                ag(ja).start()

            fy(ja).start()
            fd(ja).start()
            convert(y, c, ja)

        jy = j - lag_y

        @pl.when((jy >= 0) & (jy < NMSG))
        def _():
            fy_in(jy).wait_recv()
            fe(jy).start()
            convert(yo, c, jy)

        return carry

    lax.fori_loop(0, start + NMSG + lag_y, tick, 0)

    def out_copy(h, r):
        at = pl.ds(h * 128 + r * 32, 32)
        return pltpu.make_async_copy(obuf.at[at], out_hbm.at[at], s_out.at[h, r])

    def last(j, carry):
        fd_in(j).wait_recv()
        fe_in(j).wait_recv()
        convert(y, co, j)
        convert(yo, co, j)

        @pl.when(j % QCH == QCH - 1)
        def _():
            out_copy(0, j // QCH).start()
            out_copy(1, j // QCH).start()

        return carry

    lax.fori_loop(0, NMSG, last, 0)

    def drain(j, carry):
        @pl.when(u < 3)
        def _():
            rs(j).wait_send()

        @pl.when(u > 0)
        def _():
            ag(j).wait_send()

        fy(j).wait_send()
        fd(j).wait_send()
        fe(j).wait_send()
        return carry

    lax.fori_loop(0, NMSG, drain, 0)
    for i in range(STEPS):
        to_partner(i).wait_send()
    for r in range(RCH):
        to_across(r).wait_send()
        ctx_copy(r).wait_send()
        out_copy(0, r).wait()
        out_copy(1, r).wait()


def block(lengths, q, k_new, v_new, k_cache, v_cache, hidden, w_o):
    batch, positions, kv, head = k_cache.shape
    rows, width = hidden.shape
    depth = w_o.shape[0]
    half = width // 2
    cols = half // QCH
    dma = pltpu.SemaphoreType.DMA
    part = pltpu.VMEM((RCH, 2, 104, 128), F32)
    cache = pltpu.VMEM((SLOTS, 32, positions * kv, head), BF16)
    return pl.pallas_call(
        functools.partial(block_kernel, positions=positions, scale=head ** -0.5),
        out_shape=jax.ShapeDtypeStruct((rows, width), BF16),
        in_specs=[pl.BlockSpec(memory_space=pltpu.SMEM), VMEM, VMEM, VMEM, ANY, ANY, ANY, ANY],
        out_specs=ANY,
        scratch_shapes=[cache, cache,
                        pltpu.VMEM((512, positions * kv), F32), pltpu.VMEM((512, 16), F32),
                        pltpu.VMEM((512, positions * kv), BF16), pltpu.VMEM((512, 128), F32),
                        pltpu.VMEM((STEPS, 4, 104, 128), F32), pltpu.VMEM((STEPS, 2, 104, 128), F32),
                        part, part, part,
                        pltpu.VMEM((96, 128), F32),
                        pltpu.VMEM((RCH, 16, depth), F32), pltpu.VMEM((RCH, 16, depth), F32),
                        pltpu.VMEM((2, 16, depth), BF16),
                        pltpu.VMEM((QCH, depth, cols), BF16),
                        pltpu.VMEM((rows // 2, half), BF16),
                        pltpu.VMEM((32, cols), F32),
                        pltpu.VMEM((NMSG, 32, cols), F32), pltpu.VMEM((NMSG, 32, cols), F32),
                        pltpu.VMEM((2, 2, NMSG, 32, cols), F32),
                        pltpu.VMEM((rows, width), BF16),
                        dma((SLOTS,)), dma((SLOTS,)), dma((STEPS,)), dma((STEPS,)), dma((RCH,)), dma((RCH,)),
                        dma((RCH,)), dma((RCH,)), dma((QCH,)), dma] + [dma((NMSG,))] * 10 + [dma((2, RCH))],
        compiler_params=pltpu.CompilerParams(collective_id=0, has_side_effects=True, vmem_limit_bytes=VMEM_LIMIT),
        name="block",
    )(lengths, q, k_new, v_new, k_cache.reshape(batch, positions * kv, head), v_cache.reshape(batch, positions * kv, head), hidden, w_o)


def solution(mesh):
    def local_step(hidden, ln_gain, ln_bias, w_q, w_k, w_v, w_o, k_cache, v_cache, lengths):
        batch, _, kv, head = k_cache.shape
        q, k_new, v_new = qkv(hidden, ln_gain, ln_bias, lengths, w_q, w_k, w_v)
        out = block(lengths, q, k_new, v_new, k_cache, v_cache, hidden, w_o)
        return out, k_new.reshape(batch, kv, head), v_new.reshape(batch, kv, head)

    row_spec = P('dp', None)
    cache_spec = P('dp', 'sp', 'tp', None)
    head_spec = P('dp', 'tp', None)
    return jax.shard_map(local_step, mesh=mesh, in_specs=(row_spec, P(None), P(None), P(None, 'tp'), P(None, 'tp'), P(None, 'tp'), P('tp', None), cache_spec, cache_spec, P('dp')), out_specs=(row_spec, head_spec, head_spec), check_vma=False)
```

time: 136 us -> 93 us (0.68)
  the two profiles are of different devices: /device:TPU:0 before, /device:TPU:31 now
where the time goes in v3:
time: 93 us; the launch traced here: 92.8 us
  Pallas kernels  88.2 us (95%)
  local copies, waits for them, and re-layouts  3.88 us (4%)
    pallas_call x1, Pallas kernels, block(): pl.pallas_call(functools.partial(block_kernel, positions=positions, scale...  71.4 us
    pallas_call x1, Pallas kernels, qkv(): pl.pallas_call(qkv_kernel, out_shape=(jax.ShapeDtypeStruct((rows * 16, 12...  16.8 us
    unnamed x1, local copies, waits for them, and re-layouts  3.88 us

profile of v3, /device:TPU:31, one launch (start us, length us, event | category | flops | bytes accessed | tf_op | source)
XLA Modules:
  0.0 92.8 jit_solution(7780103554197270062)
XLA Ops:
  0.6 16.8 %qkv.1 = (bf16[4096,128]{1,0:T(8,128)(2,1)}, bf16[512,128]{1,0:T(8,128)(2,1)}, bf16[512,128]{1,0:T(8,128)(2,1)}) custom-call(s32[2,128]{1,0:T(2,128)} %bitcast.13, f32[1,128]{1,0:T(1,128)} %constant.2.clone.freq_ref, bf16[48,128]{1,0:T(8,128)(2,1)} %bitcast.11, bf16[48,128]{1,0:T(8,128)(2,1)} %bitcast.12, bf16[256,6144]{1,0:T(8,128)(2,1)} %x_hbm.3, ...), custom_call_target="tpu_custom_call" | custom-call | tf_op jit(solution)/shard_map/qkv/pallas_call | solution.py:116
  17.4 71.4 %block.1 = bf16[256,6144]{1,0:T(8,128)(2,1)} custom-call(s32[256]{0:T(256)} %len_ref.1, bf16[4096,128]{1,0:T(8,128)(2,1)} %get-tuple-element.6.q_ref, bf16[512,128]{1,0:T(8,128)(2,1)} %get-tuple-element.7.kn_ref, bf16[512,128]{1,0:T(8,128)(2,1)} %get-tuple-element.8.vn_ref, bf16[256,256,128]{2,1,0:T(8,128)(2,1)} %bitcast.7, bf16[256,256,128]{2,1,0:T(8,128)(2,1)} %bitcast.8, ...), custom_call_target="tpu_custom_call" | custom-call | tf_op jit(solution)/shard_map/block/pallas_call | solution.py:480
  88.9 3.9 %copy.15 = bf16[256,6144]{1,0:T(8,128)(2,1)} copy(bf16[256,6144]{1,0:T(8,128)(2,1)} %block.1) | data formatting | bytes 6291456

commit v4 on v3

--- a/solution.py
+++ b/solution.py
@@ -12,124 +12,9 @@
 BF16 = jnp.bfloat16
 MESH = pl.DeviceIdType.MESH
 NEG = -0.7 * float(np.finfo(np.float32).max)
-VMEM_LIMIT = 60 * 1024 * 1024
+BLOCK_LIMIT = 49 * 1024 * 1024
 ANY = pl.BlockSpec(memory_space=pl.ANY)
 VMEM = pl.BlockSpec(memory_space=pltpu.VMEM)
-
-
-def qkv_kernel(len_ref, freq_ref, gain_ref, bias_ref, x_hbm, wq_hbm, wk_hbm, wv_hbm,
-               q_out, k_out, v_out, xbuf, hbuf, wbuf, pbuf, qf, kf, cosb, sinb, gainb, biasb, xsem, wsem):
-    rows, width = xbuf.shape
-    n_q = wq_hbm.shape[1] // 256
-    tiles = width // 128
-
-    x_copy = pltpu.make_async_copy(x_hbm, xbuf, xsem)
-    x_copy.start()
-
-    def q_copy(i):
-        return pltpu.make_async_copy(wq_hbm.at[:, pl.ds(i * 256, 256)], wbuf.at[i], wsem.at[i])
-
-    k_copy = pltpu.make_async_copy(wk_hbm, wbuf.at[n_q], wsem.at[n_q])
-    v_copy = pltpu.make_async_copy(wv_hbm, wbuf.at[n_q + 1], wsem.at[n_q + 1])
-    for k in range(tiles):
-        gainb[:, k * 128:(k + 1) * 128] = jnp.broadcast_to(1.0 + gain_ref[k:k + 1, :].astype(F32), (8, 128))
-        biasb[:, k * 128:(k + 1) * 128] = jnp.broadcast_to(bias_ref[k:k + 1, :].astype(F32), (8, 128))
-    for i in range(rows // 128):
-        place = jnp.transpose(jnp.broadcast_to(len_ref[i:i + 1, :].astype(F32), (128, 128)))
-        angle = place * freq_ref[...]
-        cosb[i * 128:(i + 1) * 128, :] = jnp.cos(angle)
-        sinb[i * 128:(i + 1) * 128, :] = jnp.sin(angle)
-
-    x_copy.wait()
-    q_copy(0).start()
-    q_copy(1).start()
-
-    def norm(i, carry):
-        @pl.when(i < n_q - 2)
-        def _():
-            q_copy(i + 2).start()
-
-        ats = [pl.ds(pl.multiple_of(i * 64 + j * 16, 16), 16) for j in range(4)]
-        lanes = [slice(k * 128, (k + 1) * 128) for k in range(tiles)]
-        means, scales = [], []
-        for at in ats:
-            accs = [xbuf[at, lanes[k]].astype(F32) for k in range(2)]
-            for k in range(2, tiles):
-                accs[k % 2] = accs[k % 2] + xbuf[at, lanes[k]].astype(F32)
-            mean = jnp.sum(accs[0] + accs[1], axis=-1, keepdims=True) * (1.0 / width)
-            means.append(jnp.broadcast_to(mean, (16, 128)))
-        for at, mean in zip(ats, means):
-            accs = [jnp.zeros((16, 128), F32) for _ in range(2)]
-            for k in range(tiles):
-                centred = xbuf[at, lanes[k]].astype(F32) - mean
-                accs[k % 2] = accs[k % 2] + centred * centred
-            var = jnp.sum(accs[0] + accs[1], axis=-1, keepdims=True) * (1.0 / width)
-            scales.append(jnp.broadcast_to(lax.rsqrt(var + 1e-5), (16, 128)))
-        for k in range(tiles):
-            gain = jnp.concatenate([gainb[:, lanes[k]]] * 2, axis=0)
-            bias = jnp.concatenate([biasb[:, lanes[k]]] * 2, axis=0)
-            for at, mean, scale in zip(ats, means, scales):
-                hbuf[at, lanes[k]] = ((xbuf[at, lanes[k]].astype(F32) - mean) * scale * gain + bias).astype(BF16)
-        return carry
-
-    lax.fori_loop(0, rows // 64, norm, 0)
-    k_copy.start()
-    v_copy.start()
-
-    lane = lax.broadcasted_iota(jnp.int32, (rows, 128), 1)
-
-    def rotate(u):
-        other = jnp.where(lane < 32, -pltpu.roll(u, 96, 1), pltpu.roll(u, 32, 1))
-        turned = u * cosb[...] + other * sinb[...]
-        return jnp.where(lane < 64, turned, u)
-
-    def project(i):
-        return jnp.dot(hbuf[...], wbuf[i], preferred_element_type=F32)
-
-    def place_heads(i, prod):
-        for head in range(2):
-            u = prod[:, head * 128:(head + 1) * 128]
-            qf[pl.ds(lax.rem(2 * i + head, 16), rows, stride=16), :] = jnp.where(i == n_q + 1, u, rotate(u))
-
-    pbuf[1] = jnp.zeros((rows, 256), F32)
-
-    def tile(i, carry):
-        pltpu.make_async_copy(wk_hbm, wbuf.at[i], wsem.at[i]).wait()
-        pbuf[lax.rem(i, 2)] = project(i)
-        place_heads(i + n_q + 1, pbuf[lax.rem(i + 1, 2)])
-        return carry
-
-    lax.fori_loop(0, n_q + 2, tile, 0)
-    place_heads(n_q + 1, pbuf[(n_q + 1) % 2])
-    for ref, row in ((k_out, 12), (v_out, 14)):
-        for head in range(2):
-            kf[pl.ds(head, rows, stride=2), :] = qf[pl.ds(row + head, rows, stride=16), :]
-        ref[...] = kf[...].astype(BF16)
-    q_out[...] = qf[...].astype(BF16)
-
-
-def qkv(hidden, gain, bias, lengths, w_q, w_k, w_v):
-    rows, width = hidden.shape
-    n_tiles = w_q.shape[1] // 256 + 2
-    freq = 10000.0 ** (-2.0 * np.arange(32, dtype=np.float32) / np.float32(64))
-    freq = np.concatenate([freq, freq, np.zeros(64)]).astype(np.float32).reshape(1, 128)
-    return pl.pallas_call(
-        qkv_kernel,
-        out_shape=(jax.ShapeDtypeStruct((rows * 16, 128), BF16),
-                   jax.ShapeDtypeStruct((rows * 2, 128), BF16),
-                   jax.ShapeDtypeStruct((rows * 2, 128), BF16)),
-        in_specs=[VMEM, VMEM, VMEM, VMEM, ANY, ANY, ANY, ANY],
-        out_specs=(VMEM, VMEM, VMEM),
-        scratch_shapes=[pltpu.VMEM((rows, width), BF16), pltpu.VMEM((rows, width), BF16),
-                        pltpu.VMEM((n_tiles, width, 256), BF16), pltpu.VMEM((2, rows, 256), F32),
-                        pltpu.VMEM((rows * 16, 128), F32), pltpu.VMEM((rows * 2, 128), F32),
-                        pltpu.VMEM((rows, 128), F32), pltpu.VMEM((rows, 128), F32),
-                        pltpu.VMEM((8, width), F32), pltpu.VMEM((8, width), F32),
-                        pltpu.SemaphoreType.DMA, pltpu.SemaphoreType.DMA((n_tiles,))],
-        compiler_params=pltpu.CompilerParams(vmem_limit_bytes=VMEM_LIMIT),
-        name="qkv",
-    )(lengths.reshape(rows // 128, 128), jnp.asarray(freq), gain.reshape(width // 128, 128),
-      bias.reshape(width // 128, 128), hidden, w_q, w_k, w_v)
 
 
 RCH = 4
@@ -153,19 +38,21 @@
     return acc, top, total, turned[:96, 2:3]
 
 
-def block_kernel(len_ref, q_ref, kn_ref, vn_ref, k_hbm, v_hbm, x_hbm, w_hbm, out_hbm,
+def block_kernel(len_ref, len_rows, freq_ref, gain_ref, bias_ref, x_hbm, wq_hbm, wk_hbm, wv_hbm, k_hbm, v_hbm, w_hbm,
+                 obuf, kn_ref, vn_ref,
+                 hbuf, acc_ref, q_ref, kf, vf, xs, xr, cosb, sinb, gainb, biasb, s_h, s_q, s_g, s_xs, r_xs,
                  kbuf, vbuf, sbuf, self_buf, pbuf, stat, msg, part, send_y, recv_y, comb_o, ctx_t, ctx_s, ctx_r,
-                 lhs, wbuf, xbuf, prod, rs_in, rs_out, fin, obuf,
+                 lhs, wbuf, xbuf, prod, rs_in, rs_out, fin,
                  s_k, s_v, s_p, r_p, s_y, r_y, s_c, r_c, s_w, s_x,
-                 s_rs, r_rs, s_ag, r_ag, s_fy, r_fy, s_fd, r_fd, s_fe, r_fe, s_out, *, positions, scale):
+                 s_rs, r_rs, s_ag, r_ag, s_fy, r_fy, s_fd, r_fd, s_fe, r_fe, *, positions, scale):
     d, z, s = lax.axis_index("dp"), lax.axis_index("tp"), lax.axis_index("sp")
     y, c = s // 2, s % 2
     yo, co = 1 - y, 1 - c
     u = c * z + co * (3 - z)
     partner, across = (d, z, 2 * y + co), (d, z, 2 * yo + c)
     ahead, behind = (d, z + 2 * c - 1, s), (d, z - 2 * c + 1, s)
-    half = wbuf.shape[0] * wbuf.shape[2]
     width = wbuf.shape[2]
+    half = QCH * width
 
     def remote(src, dst, send, recv, dev):
         return pltpu.make_async_remote_copy(src_ref=src, dst_ref=dst, send_sem=send, recv_sem=recv,
@@ -197,11 +84,113 @@
 
     x_copy = pltpu.make_async_copy(x_hbm.at[pl.ds(y * 128, 128), pl.ds(c * half, half)], xbuf, s_x)
 
+    rows, model = hbuf.shape
+    tiles = model // 128
+    depth = wbuf.shape[1]
+    h_copy = pltpu.make_async_copy(x_hbm, obuf, s_h)
+    h_copy.start()
+
+    def q_copy(n):
+        return pltpu.make_async_copy(wq_hbm.at[pl.ds(n * depth, depth), pl.ds(c * 768, 512)], wbuf.at[n], s_q.at[n])
+
+    def g_copies(n):
+        at = pl.ds(n * depth, depth)
+        return [pltpu.make_async_copy(wq_hbm.at[at, pl.ds(c * 768 + 512, 256)], wbuf.at[4 + n, :, pl.ds(0, 256)], s_g.at[0, n]),
+                pltpu.make_async_copy(wk_hbm.at[at, pl.ds(c * 128, 128)], wbuf.at[4 + n, :, pl.ds(256, 128)], s_g.at[1, n]),
+                pltpu.make_async_copy(wv_hbm.at[at, pl.ds(c * 128, 128)], wbuf.at[4 + n, :, pl.ds(384, 128)], s_g.at[2, n])]
+
+    def share(g):
+        at = pl.ds(4 * g, 4)
+        return remote(xs.at[at], xr.at[at], s_xs.at[g], r_xs.at[g], partner)
+
+    for k in range(tiles):
+        gainb[:, k * 128:(k + 1) * 128] = jnp.broadcast_to(1.0 + gain_ref[k:k + 1, :].astype(F32), (8, 128))
+        biasb[:, k * 128:(k + 1) * 128] = jnp.broadcast_to(bias_ref[k:k + 1, :].astype(F32), (8, 128))
+    for i in range(rows // 128):
+        angle = jnp.transpose(jnp.broadcast_to(len_rows[i:i + 1, :].astype(F32), (128, 128))) * freq_ref[...]
+        cosb[i * 128:(i + 1) * 128, :] = jnp.cos(angle)
+        sinb[i * 128:(i + 1) * 128, :] = jnp.sin(angle)
+    h_copy.wait()
+    for n in range(4):
+        q_copy(n).start()
+
+    def norm(i, carry):
+        for copy in g_copies(i):
+            copy.start()
+        ats = [pl.ds(pl.multiple_of(i * 64 + j * 16, 16), 16) for j in range(4)]
+        lanes = [slice(k * 128, (k + 1) * 128) for k in range(tiles)]
+        means, scales = [], []
+        for at in ats:
+            accs = [obuf[at, lanes[k]].astype(F32) for k in range(2)]
+            for k in range(2, tiles):
+                accs[k % 2] = accs[k % 2] + obuf[at, lanes[k]].astype(F32)
+            mean = jnp.sum(accs[0] + accs[1], axis=-1, keepdims=True) * (1.0 / model)
+            means.append(jnp.broadcast_to(mean, (16, 128)))
+        for at, mean in zip(ats, means):
+            accs = [jnp.zeros((16, 128), F32) for _ in range(2)]
+            for k in range(tiles):
+                centred = obuf[at, lanes[k]].astype(F32) - mean
+                accs[k % 2] = accs[k % 2] + centred * centred
+            var = jnp.sum(accs[0] + accs[1], axis=-1, keepdims=True) * (1.0 / model)
+            scales.append(jnp.broadcast_to(lax.rsqrt(var + 1e-5), (16, 128)))
+        for k in range(tiles):
+            gain = jnp.concatenate([gainb[:, lanes[k]]] * 2, axis=0)
+            bias = jnp.concatenate([biasb[:, lanes[k]]] * 2, axis=0)
+            for at, mean, factor in zip(ats, means, scales):
+                hbuf[at, lanes[k]] = ((obuf[at, lanes[k]].astype(F32) - mean) * factor * gain + bias).astype(BF16)
+        return carry
+
+    lax.fori_loop(0, rows // 64, norm, 0)
     for i in range(SLOTS):
         k_copy(i).start()
         v_copy(i).start()
     x_copy.start()
-    pl.semaphore_wait(barrier, 2 + (z + 2) // 3 + (5 - z) // 3)
+
+    lane_r = lax.broadcasted_iota(jnp.int32, (rows, 128), 1)
+
+    def rotate(v):
+        other = jnp.where(lane_r < 32, -pltpu.roll(v, 96, 1), pltpu.roll(v, 32, 1))
+        return jnp.where(lane_r < 64, v * cosb[...] + other * sinb[...], v)
+
+    def spread_out(slot, core, v):
+        if slot < 6:
+            q_ref[pl.ds(6 * core + slot, rows, stride=16), :] = v
+        else:
+            dst = kf if slot == 6 else vf
+            dst[pl.ds(core, rows, stride=2), :] = v
+
+    for h in range(12, 16):
+        q_ref[pl.ds(h, rows, stride=16), :] = jnp.zeros((rows, 128), F32)
+
+    for g in range(2):
+        acc_ref[...] = jnp.zeros_like(acc_ref)
+
+        def accumulate(n, carry):
+            if g == 0:
+                q_copy(n).wait()
+            else:
+                for copy in g_copies(n):
+                    copy.wait()
+            left = hbuf[:, pl.ds(pl.multiple_of(n * depth, 128), depth)]
+            acc_ref[...] += jnp.dot(left, wbuf[4 * g + n], preferred_element_type=F32)
+            return carry
+
+        lax.fori_loop(0, 4, accumulate, 0)
+        if g == 0:
+            pl.semaphore_wait(barrier, 2 + (z + 2) // 3 + (5 - z) // 3)
+        for n in range(4):
+            v = acc_ref[:, n * 128:(n + 1) * 128]
+            if 4 * g + n < 7:
+                v = rotate(v)
+            xs[4 * g + n] = v
+            spread_out(4 * g + n, c, v)
+        share(g).start()
+    for g in range(2):
+        share(g).wait_recv()
+        for n in range(4):
+            spread_out(4 * g + n, co, xr[4 * g + n])
+    kn_ref[...] = kf[...].astype(BF16)
+    vn_ref[...] = vf[...].astype(BF16)
 
     first = s * positions
     col = lax.broadcasted_iota(jnp.int32, (16, 2 * positions), 1)
@@ -223,7 +212,7 @@
         own_w = [None] * 4
 
         def scores(g):
-            q8 = q_ref[pl.ds(pl.multiple_of(base * 16 + g * 128, 128), 128), :]
+            q8 = q_ref[pl.ds(pl.multiple_of(base * 16 + g * 128, 128), 128), :].astype(BF16)
             kn = kn_ref[pl.ds(pl.multiple_of(base * 2 + g * 16, 16), 16), :]
             self8 = lax.dot_general(q8, kn, nt, preferred_element_type=F32) * scale
             self8 = jnp.where(pick, self8, NEG)
@@ -425,21 +414,11 @@
 
     lax.fori_loop(0, start + NMSG + lag_y, tick, 0)
 
-    def out_copy(h, r):
-        at = pl.ds(h * 128 + r * 32, 32)
-        return pltpu.make_async_copy(obuf.at[at], out_hbm.at[at], s_out.at[h, r])
-
     def last(j, carry):
         fd_in(j).wait_recv()
         fe_in(j).wait_recv()
         convert(y, co, j)
         convert(yo, co, j)
-
-        @pl.when(j % QCH == QCH - 1)
-        def _():
-            out_copy(0, j // QCH).start()
-            out_copy(1, j // QCH).start()
-
         return carry
 
     lax.fori_loop(0, NMSG, last, 0)
@@ -459,30 +438,40 @@
         return carry
 
     lax.fori_loop(0, NMSG, drain, 0)
+    for g in range(2):
+        share(g).wait_send()
     for i in range(STEPS):
         to_partner(i).wait_send()
     for r in range(RCH):
         to_across(r).wait_send()
         ctx_copy(r).wait_send()
-        out_copy(0, r).wait()
-        out_copy(1, r).wait()
-
-
-def block(lengths, q, k_new, v_new, k_cache, v_cache, hidden, w_o):
+
+
+def block(lengths, gain, bias, hidden, w_q, w_k, w_v, k_cache, v_cache, w_o):
     batch, positions, kv, head = k_cache.shape
     rows, width = hidden.shape
     depth = w_o.shape[0]
     half = width // 2
     cols = half // QCH
+    freq = 10000.0 ** (-2.0 * np.arange(32, dtype=np.float32) / np.float32(64))
+    freq = np.concatenate([freq, freq, np.zeros(64)]).astype(np.float32).reshape(1, 128)
     dma = pltpu.SemaphoreType.DMA
     part = pltpu.VMEM((RCH, 2, 104, 128), F32)
     cache = pltpu.VMEM((SLOTS, 32, positions * kv, head), BF16)
+    table = pltpu.VMEM((rows, 128), F32)
+    pair = pltpu.VMEM((rows * 2, 128), F32)
+    shared = pltpu.VMEM((8, rows, 128), F32)
+    line = pltpu.VMEM((8, width), F32)
+    new = jax.ShapeDtypeStruct((rows * kv, head), BF16)
     return pl.pallas_call(
         functools.partial(block_kernel, positions=positions, scale=head ** -0.5),
-        out_shape=jax.ShapeDtypeStruct((rows, width), BF16),
-        in_specs=[pl.BlockSpec(memory_space=pltpu.SMEM), VMEM, VMEM, VMEM, ANY, ANY, ANY, ANY],
-        out_specs=ANY,
-        scratch_shapes=[cache, cache,
+        out_shape=(jax.ShapeDtypeStruct((rows, width), BF16), new, new),
+        in_specs=[pl.BlockSpec(memory_space=pltpu.SMEM), VMEM, VMEM, VMEM, VMEM] + [ANY] * 7,
+        out_specs=(VMEM, VMEM, VMEM),
+        scratch_shapes=[pltpu.VMEM((rows, width), BF16), pltpu.VMEM((rows, 512), F32), pltpu.VMEM((rows * 16, 128), F32),
+                        pair, pair, shared, shared, table, table, line, line,
+                        dma, dma((4,)), dma((3, 4)), dma((2,)), dma((2,)),
+                        cache, cache,
                         pltpu.VMEM((512, positions * kv), F32), pltpu.VMEM((512, 16), F32),
                         pltpu.VMEM((512, positions * kv), BF16), pltpu.VMEM((512, 128), F32),
                         pltpu.VMEM((STEPS, 4, 104, 128), F32), pltpu.VMEM((STEPS, 2, 104, 128), F32),
@@ -490,24 +479,23 @@
                         pltpu.VMEM((96, 128), F32),
                         pltpu.VMEM((RCH, 16, depth), F32), pltpu.VMEM((RCH, 16, depth), F32),
                         pltpu.VMEM((2, 16, depth), BF16),
-                        pltpu.VMEM((QCH, depth, cols), BF16),
+                        pltpu.VMEM((8, depth, cols), BF16),
                         pltpu.VMEM((rows // 2, half), BF16),
                         pltpu.VMEM((32, cols), F32),
                         pltpu.VMEM((NMSG, 32, cols), F32), pltpu.VMEM((NMSG, 32, cols), F32),
                         pltpu.VMEM((2, 2, NMSG, 32, cols), F32),
-                        pltpu.VMEM((rows, width), BF16),
                         dma((SLOTS,)), dma((SLOTS,)), dma((STEPS,)), dma((STEPS,)), dma((RCH,)), dma((RCH,)),
-                        dma((RCH,)), dma((RCH,)), dma((QCH,)), dma] + [dma((NMSG,))] * 10 + [dma((2, RCH))],
-        compiler_params=pltpu.CompilerParams(collective_id=0, has_side_effects=True, vmem_limit_bytes=VMEM_LIMIT),
+                        dma((RCH,)), dma((RCH,)), dma((QCH,)), dma] + [dma((NMSG,))] * 10,
+        compiler_params=pltpu.CompilerParams(collective_id=0, has_side_effects=True, vmem_limit_bytes=BLOCK_LIMIT),
         name="block",
-    )(lengths, q, k_new, v_new, k_cache.reshape(batch, positions * kv, head), v_cache.reshape(batch, positions * kv, head), hidden, w_o)
+    )(lengths, lengths.reshape(rows // 128, 128), jnp.asarray(freq), gain.reshape(width // 128, 128), bias.reshape(width // 128, 128),
+      hidden, w_q, w_k, w_v, k_cache.reshape(batch, positions * kv, head), v_cache.reshape(batch, positions * kv, head), w_o)
 
 
 def solution(mesh):
     def local_step(hidden, ln_gain, ln_bias, w_q, w_k, w_v, w_o, k_cache, v_cache, lengths):
         batch, _, kv, head = k_cache.shape
-        q, k_new, v_new = qkv(hidden, ln_gain, ln_bias, lengths, w_q, w_k, w_v)
-        out = block(lengths, q, k_new, v_new, k_cache, v_cache, hidden, w_o)
+        out, k_new, v_new = block(lengths, ln_gain, ln_bias, hidden, w_q, w_k, w_v, k_cache, v_cache, w_o)
         return out, k_new.reshape(batch, kv, head), v_new.reshape(batch, kv, head)
 
     row_spec = P('dp', None)

time: 93 us -> 87.8 us (0.944)
  the two profiles are of different devices: /device:TPU:31 before, /device:TPU:29 now
where the time goes in v4:
time: 87.8 us; the launch traced here: 87.5 us
  Pallas kernels  81.1 us (92%)
  local copies, waits for them, and re-layouts  5.72 us (7%)
    pallas_call x1, Pallas kernels, block(): pl.pallas_call(functools.partial(block_kernel, positions=positions, scale...  81.1 us
    unnamed x11, local copies, waits for them, and re-layouts  5.72 us

profile of v4, /device:TPU:29, one launch (start us, length us, event | category | flops | bytes accessed | tf_op | source)
XLA Modules:
  0.0 87.5 jit_solution(6830585242659863051)
XLA Ops:
  0.6 0.0 copy-start
  0.6 0.7 copy-done
  1.3 0.0 copy-start.1
  1.3 0.7 copy-done.1
  2.0 0.0 copy-start.2
  2.1 0.7 copy-done.2
  2.7 0.0 copy-start.3
  2.7 0.7 copy-done.3
  3.4 81.1 %block.1 = (bf16[256,6144]{1,0:T(8,128)(2,1)S(1)}, bf16[512,128]{1,0:T(8,128)(2,1)S(1)}, bf16[512,128]{1,0:T(8,128)(2,1)S(1)}) custom-call(s32[256]{0:T(256)S(1)} %copy-done.2, s32[2,128]{1,0:T(2,128)S(1)} %bitcast.11, f32[1,128]{1,0:T(1,128)S(1)} %copy-done.3, bf16[48,128]{1,0:T(8,128)(2,1)S(1)} %bitcast.9, bf16[48,128]{1,0:T(8,128)(2,1)S(1)} %bitcast.10, ...), custom_call_target="tpu_custom_call" | custom-call | tf_op jit(solution)/shard_map/block/pallas_call | solution.py:466
  84.5 1.7 %copy.17 = bf16[256,6144]{1,0:T(8,128)(2,1)} copy(bf16[256,6144]{1,0:T(8,128)(2,1)S(1)} %get-tuple-element.12) | data formatting | bytes 6291456
  86.2 0.7 copy.18
  86.8 0.7 copy.19
Async XLA Ops:
  0.6 0.7 copy-start
  1.3 0.7 copy-start.1
  2.0 0.7 copy-start.2
  2.7 0.7 copy-start.3

commit v5 on v4

--- a/solution.py
+++ b/solution.py
@@ -13,7 +13,7 @@
 MESH = pl.DeviceIdType.MESH
 NEG = -0.7 * float(np.finfo(np.float32).max)
 BLOCK_LIMIT = 49 * 1024 * 1024
-ANY = pl.BlockSpec(memory_space=pl.ANY)
+HBM = pl.BlockSpec(memory_space=pltpu.HBM)
 VMEM = pl.BlockSpec(memory_space=pltpu.VMEM)
 
 
@@ -23,7 +23,8 @@
 PER = QCH // 2
 STEPS = 2 * RCH
 HOP = 3
-LAG = 6
+LAG = 5
+LAG_Y = 6
 SLOTS = 3
 
 
@@ -38,13 +39,14 @@
     return acc, top, total, turned[:96, 2:3]
 
 
-def block_kernel(len_ref, len_rows, freq_ref, gain_ref, bias_ref, x_hbm, wq_hbm, wk_hbm, wv_hbm, k_hbm, v_hbm, w_hbm,
+def block_kernel(len_hbm, freq_hbm, gain_hbm, bias_hbm, x_hbm, wq_hbm, wk_hbm, wv_hbm, k_hbm, v_hbm, w_hbm,
                  obuf, kn_ref, vn_ref,
+                 len_ref, len_rows, freq_ref, gain_ref, bias_ref, s_in,
                  hbuf, acc_ref, q_ref, kf, vf, xs, xr, cosb, sinb, gainb, biasb, s_h, s_q, s_g, s_xs, r_xs,
                  kbuf, vbuf, sbuf, self_buf, pbuf, stat, msg, part, send_y, recv_y, comb_o, ctx_t, ctx_s, ctx_r,
                  lhs, wbuf, xbuf, prod, rs_in, rs_out, fin,
                  s_k, s_v, s_p, r_p, s_y, r_y, s_c, r_c, s_w, s_x,
-                 s_rs, r_rs, s_ag, r_ag, s_fy, r_fy, s_fd, r_fd, s_fe, r_fe, *, positions, scale):
+                 s_rs, r_rs, r_re, s_ag, r_ag, s_ae, s_fy, r_fy, s_fd, r_fd, s_fe, r_fe, *, positions, scale):
     d, z, s = lax.axis_index("dp"), lax.axis_index("tp"), lax.axis_index("sp")
     y, c = s // 2, s % 2
     yo, co = 1 - y, 1 - c
@@ -88,6 +90,10 @@
     tiles = model // 128
     depth = wbuf.shape[1]
     h_copy = pltpu.make_async_copy(x_hbm, obuf, s_h)
+    inputs = ((len_hbm, len_ref), (len_hbm, len_rows), (freq_hbm, freq_ref), (gain_hbm, gain_ref), (bias_hbm, bias_ref))
+    small = [pltpu.make_async_copy(src, dst, s_in.at[n]) for n, (src, dst) in enumerate(inputs)]
+    for copy in small:
+        copy.start()
     h_copy.start()
 
     def q_copy(n):
@@ -103,6 +109,8 @@
         at = pl.ds(4 * g, 4)
         return remote(xs.at[at], xr.at[at], s_xs.at[g], r_xs.at[g], partner)
 
+    for copy in small:
+        copy.wait()
     for k in range(tiles):
         gainb[:, k * 128:(k + 1) * 128] = jnp.broadcast_to(1.0 + gain_ref[k:k + 1, :].astype(F32), (8, 128))
         biasb[:, k * 128:(k + 1) * 128] = jnp.broadcast_to(bias_ref[k:k + 1, :].astype(F32), (8, 128))
@@ -218,7 +226,7 @@
             self8 = jnp.where(pick, self8, NEG)
             for b in range(8):
                 at = slice(g * 128 + b * 16, g * 128 + (b + 1) * 16)
-                length = len_ref[base + g * 8 + b]
+                length = len_ref[base // 128, base % 128 + g * 8 + b]
                 owner = (length >= begin) & (length < begin + positions)
                 sc = lax.dot_general(q8[b * 16:(b + 1) * 16, :], kbuf[slot, g * 8 + b], nt, preferred_element_type=F32) * scale
                 sbuf[at, :] = jnp.where(place < length, sc, NEG)
@@ -282,6 +290,9 @@
     def rs(j):
         return remote(rs_out.at[j], rs_in.at[j], s_rs.at[j], r_rs.at[j], ahead)
 
+    def rs_end(j):
+        return remote(rs_out.at[j], fin.at[y, c, j], s_rs.at[j], r_re.at[j], behind)
+
     def final(dst, send, recv, h, core, j):
         f = fin.at[h, core, j]
         return remote(f, f, send.at[j], recv.at[j], dst)
@@ -289,6 +300,9 @@
     def ag(j):
         return final(behind, s_ag, r_ag, y, c, j)
 
+    def ag_end(j):
+        return final(ahead, s_ae, r_ag, y, c, j)
+
     def fy(j):
         return final(across, s_fy, r_fy, y, c, j)
 
@@ -311,9 +325,10 @@
         at = pl.ds(pl.multiple_of(h * 128 + (j // QCH) * 32, 32), 32)
         obuf[at, pl.ds(pl.multiple_of(core * half + (j % QCH) * width, width), width)] = fin[h, core, j].astype(BF16)
 
-    lag = LAG * (3 - u)
-    lag_y = lag + LAG
-    start = 2 * QCH + HOP * u
+    hops = u - 2 * (u // 3)
+    lag = LAG * (2 - hops)
+    lag_y = lag + LAG_Y
+    start = 2 * QCH + HOP * hops
 
     def tick(t, carry):
         i, r6 = t // PER, t // QCH
@@ -372,29 +387,36 @@
                 rs_out[j] = prod[...]
                 rs(j).start()
 
-            @pl.when((u > 0) & (u < 3))
+            @pl.when(u == 3)
+            def _():
+                rs_out[j] = prod[...]
+                rs_end(j).start()
+
+            @pl.when(u == 1)
             def _():
                 rs(j).wait_recv()
                 rs_out[j] = rs_in[j] + prod[...]
                 rs(j).start()
 
-            @pl.when(u == 3)
-            def _():
+            @pl.when(u == 2)
+            def _():
+                x = xbuf[pl.ds(pl.multiple_of(r * 32, 32), 32), pl.ds(pl.multiple_of(q * width, width), width)]
+                rs_end(j).wait_recv()
                 rs(j).wait_recv()
-                x = xbuf[pl.ds(pl.multiple_of(r * 32, 32), 32), pl.ds(pl.multiple_of(q * width, width), width)]
-                fin[y, c, j] = rs_in[j] + prod[...] + x.astype(F32)
+                fin[y, c, j] = (rs_in[j] + prod[...]) + fin[y, c, j] + x.astype(F32)
                 ag(j).start()
+                ag_end(j).start()
                 fy(j).start()
                 fd(j).start()
                 convert(y, c, j)
 
         ja = j - lag
 
-        @pl.when((u < 3) & (ja >= 0) & (ja < NMSG))
+        @pl.when((lag > 0) & (ja >= 0) & (ja < NMSG))
         def _():
             ag(ja).wait_recv()
 
-            @pl.when(u > 0)
+            @pl.when(u == 1)
             def _():
                 ag(ja).start()
 
@@ -424,13 +446,21 @@
     lax.fori_loop(0, NMSG, last, 0)
 
     def drain(j, carry):
-        @pl.when(u < 3)
+        @pl.when(u < 2)
         def _():
             rs(j).wait_send()
 
-        @pl.when(u > 0)
+        @pl.when(u == 3)
+        def _():
+            rs_end(j).wait_send()
+
+        @pl.when((u == 1) | (u == 2))
         def _():
             ag(j).wait_send()
+
+        @pl.when(u == 2)
+        def _():
+            ag_end(j).wait_send()
 
         fy(j).wait_send()
         fd(j).wait_send()
@@ -463,12 +493,15 @@
     shared = pltpu.VMEM((8, rows, 128), F32)
     line = pltpu.VMEM((8, width), F32)
     new = jax.ShapeDtypeStruct((rows * kv, head), BF16)
+    pin = functools.partial(pltpu.with_memory_space_constraint, memory_space=pltpu.HBM)
     return pl.pallas_call(
         functools.partial(block_kernel, positions=positions, scale=head ** -0.5),
         out_shape=(jax.ShapeDtypeStruct((rows, width), BF16), new, new),
-        in_specs=[pl.BlockSpec(memory_space=pltpu.SMEM), VMEM, VMEM, VMEM, VMEM] + [ANY] * 7,
+        in_specs=[HBM] * 11,
         out_specs=(VMEM, VMEM, VMEM),
-        scratch_shapes=[pltpu.VMEM((rows, width), BF16), pltpu.VMEM((rows, 512), F32), pltpu.VMEM((rows * 16, 128), F32),
+        scratch_shapes=[pltpu.SMEM((rows // 128, 128), jnp.int32), pltpu.VMEM((rows // 128, 128), jnp.int32), pltpu.VMEM((1, 128), F32),
+                        pltpu.VMEM((width // 128, 128), BF16), pltpu.VMEM((width // 128, 128), BF16), dma((5,)),
+                        pltpu.VMEM((rows, width), BF16), pltpu.VMEM((rows, 512), F32), pltpu.VMEM((rows * 16, 128), F32),
                         pair, pair, shared, shared, table, table, line, line,
                         dma, dma((4,)), dma((3, 4)), dma((2,)), dma((2,)),
                         cache, cache,
@@ -485,17 +518,38 @@
                         pltpu.VMEM((NMSG, 32, cols), F32), pltpu.VMEM((NMSG, 32, cols), F32),
                         pltpu.VMEM((2, 2, NMSG, 32, cols), F32),
                         dma((SLOTS,)), dma((SLOTS,)), dma((STEPS,)), dma((STEPS,)), dma((RCH,)), dma((RCH,)),
-                        dma((RCH,)), dma((RCH,)), dma((QCH,)), dma] + [dma((NMSG,))] * 10,
+                        dma((RCH,)), dma((RCH,)), dma((QCH,)), dma] + [dma((NMSG,))] * 12,
         compiler_params=pltpu.CompilerParams(collective_id=0, has_side_effects=True, vmem_limit_bytes=BLOCK_LIMIT),
         name="block",
-    )(lengths, lengths.reshape(rows // 128, 128), jnp.asarray(freq), gain.reshape(width // 128, 128), bias.reshape(width // 128, 128),
+    )(pin(lengths.reshape(rows // 128, 128)), pin(jnp.asarray(freq)), pin(gain.reshape(width // 128, 128)), pin(bias.reshape(width // 128, 128)),
       hidden, w_q, w_k, w_v, k_cache.reshape(batch, positions * kv, head), v_cache.reshape(batch, positions * kv, head), w_o)
+
+
+def emit_kernel(*refs):
+    n = len(refs) // 2
+    copies = [pltpu.make_async_copy(refs[i], refs[n + i], refs[2 * n].at[i]) for i in range(n)]
+    for copy in copies:
+        copy.start()
+    for copy in copies:
+        copy.wait()
+
+
+def emit(*values):
+    n = len(values)
+    return pl.pallas_call(
+        emit_kernel,
+        out_shape=tuple(jax.ShapeDtypeStruct(v.shape, v.dtype) for v in values),
+        in_specs=[VMEM] * n, out_specs=(HBM,) * n,
+        scratch_shapes=[pltpu.SemaphoreType.DMA((n,))],
+        compiler_params=pltpu.CompilerParams(vmem_limit_bytes=4 * 1024 * 1024),
+        name="emit",
+    )(*values)
 
 
 def solution(mesh):
     def local_step(hidden, ln_gain, ln_bias, w_q, w_k, w_v, w_o, k_cache, v_cache, lengths):
         batch, _, kv, head = k_cache.shape
-        out, k_new, v_new = block(lengths, ln_gain, ln_bias, hidden, w_q, w_k, w_v, k_cache, v_cache, w_o)
+        out, k_new, v_new = emit(*block(lengths, ln_gain, ln_bias, hidden, w_q, w_k, w_v, k_cache, v_cache, w_o))
         return out, k_new.reshape(batch, kv, head), v_new.reshape(batch, kv, head)
 
     row_spec = P('dp', None)

time: 87.8 us -> 79.8 us (0.909)
  the two profiles are of different devices: /device:TPU:29 before, /device:TPU:0 now
where the time goes in v5:
time: 79.8 us; the launch traced here: 79.6 us
  Pallas kernels  79 us (99%)
    pallas_call x1, Pallas kernels, block(): pl.pallas_call(functools.partial(block_kernel, positions=positions, scale...  77.2 us
    pallas_call x1, Pallas kernels, emit(): pl.pallas_call(emit_kernel, out_shape=tuple((jax.ShapeDtypeStruct(v.shape...  1.76 us

profile of v5, /device:TPU:0, one launch (start us, length us, event | category | flops | bytes accessed | tf_op | source)
XLA Modules:
  0.0 79.6 jit_solution(147054714023094176)
XLA Ops:
  0.6 77.2 %block.1 = (bf16[256,6144]{1,0:T(8,128)(2,1)S(1)}, bf16[512,128]{1,0:T(8,128)(2,1)S(1)}, bf16[512,128]{1,0:T(8,128)(2,1)S(1)}) custom-call(s32[2,128]{1,0:T(2,128)} %bitcast.11, f32[1,128]{1,0:T(1,128)} %constant.2.clone.freq_hbm, bf16[48,128]{1,0:T(8,128)(2,1)} %bitcast.9, bf16[48,128]{1,0:T(8,128)(2,1)} %bitcast.10, bf16[256,6144]{1,0:T(8,128)(2,1)} %x_hbm.1, ...), custom_call_target="tpu_custom_call" | custom-call | tf_op jit(solution)/shard_map/block/pallas_call | solution.py:497
  77.9 1.8 %emit.1 = (bf16[256,6144]{1,0:T(8,128)(2,1)}, bf16[512,128]{1,0:T(8,128)(2,1)}, bf16[512,128]{1,0:T(8,128)(2,1)}) custom-call(bf16[256,6144]{1,0:T(8,128)(2,1)S(1)} %get-tuple-element.9.refs_0_, bf16[512,128]{1,0:T(8,128)(2,1)S(1)} %get-tuple-element.10.refs_1_, bf16[512,128]{1,0:T(8,128)(2,1)S(1)} %get-tuple-element.11.refs_2_), custom_call_target="tpu_custom_call" | custom-call | tf_op jit(solution)/shard_map/emit/pallas_call | solution.py:539

commit v6 on v5

--- a/solution.py
+++ b/solution.py
@@ -89,12 +89,17 @@
     rows, model = hbuf.shape
     tiles = model // 128
     depth = wbuf.shape[1]
-    h_copy = pltpu.make_async_copy(x_hbm, obuf, s_h)
+
+    def h_copy(i):
+        at = pl.ds(i * 64, 64)
+        return pltpu.make_async_copy(x_hbm.at[at], obuf.at[at], s_h.at[i])
+
     inputs = ((len_hbm, len_ref), (len_hbm, len_rows), (freq_hbm, freq_ref), (gain_hbm, gain_ref), (bias_hbm, bias_ref))
     small = [pltpu.make_async_copy(src, dst, s_in.at[n]) for n, (src, dst) in enumerate(inputs)]
     for copy in small:
         copy.start()
-    h_copy.start()
+    for i in range(rows // 64):
+        h_copy(i).start()
 
     def q_copy(n):
         return pltpu.make_async_copy(wq_hbm.at[pl.ds(n * depth, depth), pl.ds(c * 768, 512)], wbuf.at[n], s_q.at[n])
@@ -105,9 +110,8 @@
                 pltpu.make_async_copy(wk_hbm.at[at, pl.ds(c * 128, 128)], wbuf.at[4 + n, :, pl.ds(256, 128)], s_g.at[1, n]),
                 pltpu.make_async_copy(wv_hbm.at[at, pl.ds(c * 128, 128)], wbuf.at[4 + n, :, pl.ds(384, 128)], s_g.at[2, n])]
 
-    def share(g):
-        at = pl.ds(4 * g, 4)
-        return remote(xs.at[at], xr.at[at], s_xs.at[g], r_xs.at[g], partner)
+    def share(slot):
+        return remote(xs.at[slot], xr.at[slot], s_xs.at[slot], r_xs.at[slot], partner)
 
     for copy in small:
         copy.wait()
@@ -118,13 +122,20 @@
         angle = jnp.transpose(jnp.broadcast_to(len_rows[i:i + 1, :].astype(F32), (128, 128))) * freq_ref[...]
         cosb[i * 128:(i + 1) * 128, :] = jnp.cos(angle)
         sinb[i * 128:(i + 1) * 128, :] = jnp.sin(angle)
-    h_copy.wait()
-    for n in range(4):
-        q_copy(n).start()
 
     def norm(i, carry):
-        for copy in g_copies(i):
-            copy.start()
+        h_copy(i).wait()
+
+        @pl.when(i < 2)
+        def _():
+            q_copy(2 * i).start()
+            q_copy(2 * i + 1).start()
+
+        @pl.when(i >= 2)
+        def _():
+            for copy in g_copies(2 * i - 4) + g_copies(2 * i - 3):
+                copy.start()
+
         ats = [pl.ds(pl.multiple_of(i * 64 + j * 16, 16), 16) for j in range(4)]
         lanes = [slice(k * 128, (k + 1) * 128) for k in range(tiles)]
         means, scales = [], []
@@ -171,32 +182,22 @@
         q_ref[pl.ds(h, rows, stride=16), :] = jnp.zeros((rows, 128), F32)
 
     for g in range(2):
-        acc_ref[...] = jnp.zeros_like(acc_ref)
-
-        def accumulate(n, carry):
-            if g == 0:
-                q_copy(n).wait()
-            else:
-                for copy in g_copies(n):
-                    copy.wait()
-            left = hbuf[:, pl.ds(pl.multiple_of(n * depth, 128), depth)]
-            acc_ref[...] += jnp.dot(left, wbuf[4 * g + n], preferred_element_type=F32)
-            return carry
-
-        lax.fori_loop(0, 4, accumulate, 0)
+        for n in range(4):
+            for copy in ([q_copy(n)] if g == 0 else g_copies(n)):
+                copy.wait()
+        parts = [jnp.dot(hbuf[:, n * depth:(n + 1) * depth], wbuf[4 * g + n], preferred_element_type=F32) for n in range(4)]
+        acc_ref[...] = (parts[0] + parts[1]) + (parts[2] + parts[3])
         if g == 0:
             pl.semaphore_wait(barrier, 2 + (z + 2) // 3 + (5 - z) // 3)
-        for n in range(4):
-            v = acc_ref[:, n * 128:(n + 1) * 128]
-            if 4 * g + n < 7:
-                v = rotate(v)
-            xs[4 * g + n] = v
-            spread_out(4 * g + n, c, v)
-        share(g).start()
-    for g in range(2):
-        share(g).wait_recv()
-        for n in range(4):
-            spread_out(4 * g + n, co, xr[4 * g + n])
+        for slot in range(4 * g, 4 * g + 4):
+            v = acc_ref[:, (slot % 4) * 128:(slot % 4 + 1) * 128]
+            xs[slot] = rotate(v) if slot < 7 else v
+            share(slot).start()
+        for slot in range(4 * g, 4 * g + 4):
+            spread_out(slot, c, xs[slot])
+    for slot in range(8):
+        share(slot).wait_recv()
+        spread_out(slot, co, xr[slot])
     kn_ref[...] = kf[...].astype(BF16)
     vn_ref[...] = vf[...].astype(BF16)
 
@@ -468,8 +469,8 @@
         return carry
 
     lax.fori_loop(0, NMSG, drain, 0)
-    for g in range(2):
-        share(g).wait_send()
+    for slot in range(8):
+        share(slot).wait_send()
     for i in range(STEPS):
         to_partner(i).wait_send()
     for r in range(RCH):
@@ -503,7 +504,7 @@
                         pltpu.VMEM((width // 128, 128), BF16), pltpu.VMEM((width // 128, 128), BF16), dma((5,)),
                         pltpu.VMEM((rows, width), BF16), pltpu.VMEM((rows, 512), F32), pltpu.VMEM((rows * 16, 128), F32),
                         pair, pair, shared, shared, table, table, line, line,
-                        dma, dma((4,)), dma((3, 4)), dma((2,)), dma((2,)),
+                        dma((4,)), dma((4,)), dma((3, 4)), dma((8,)), dma((8,)),
                         cache, cache,
                         pltpu.VMEM((512, positions * kv), F32), pltpu.VMEM((512, 16), F32),
                         pltpu.VMEM((512, positions * kv), BF16), pltpu.VMEM((512, 128), F32),

time: 79.8 us -> 79.1 us (level)
  Pallas kernels: 79 us -> 78.2 us
where the time goes in v6:
time: 79.1 us; the launch traced here: 78.9 us
  Pallas kernels  78.2 us (99%)
    pallas_call x1, Pallas kernels, block(): pl.pallas_call(functools.partial(block_kernel, positions=positions, scale...  76.4 us
    pallas_call x1, Pallas kernels, emit(): pl.pallas_call(emit_kernel, out_shape=tuple((jax.ShapeDtypeStruct(v.shape...  1.76 us

profile of v6, /device:TPU:0, one launch (start us, length us, event | category | flops | bytes accessed | tf_op | source)
XLA Modules:
  0.0 78.9 jit_solution(7982932731725421494)
XLA Ops:
  0.6 76.4 %block.1 = (bf16[256,6144]{1,0:T(8,128)(2,1)S(1)}, bf16[512,128]{1,0:T(8,128)(2,1)S(1)}, bf16[512,128]{1,0:T(8,128)(2,1)S(1)}) custom-call(s32[2,128]{1,0:T(2,128)} %bitcast.11, f32[1,128]{1,0:T(1,128)} %constant.2.clone.freq_hbm, bf16[48,128]{1,0:T(8,128)(2,1)} %bitcast.9, bf16[48,128]{1,0:T(8,128)(2,1)} %bitcast.10, bf16[256,6144]{1,0:T(8,128)(2,1)} %x_hbm.1, ...), custom_call_target="tpu_custom_call" | custom-call | tf_op jit(solution)/shard_map/block/pallas_call | solution.py:498
  77.1 1.8 %emit.1 = (bf16[256,6144]{1,0:T(8,128)(2,1)}, bf16[512,128]{1,0:T(8,128)(2,1)}, bf16[512,128]{1,0:T(8,128)(2,1)}) custom-call(bf16[256,6144]{1,0:T(8,128)(2,1)S(1)} %get-tuple-element.9.refs_0_, bf16[512,128]{1,0:T(8,128)(2,1)S(1)} %get-tuple-element.10.refs_1_, bf16[512,128]{1,0:T(8,128)(2,1)S(1)} %get-tuple-element.11.refs_2_), custom_call_target="tpu_custom_call" | custom-call | tf_op jit(solution)/shard_map/emit/pallas_call | solution.py:540

commit v7 on v6

--- a/solution.py
+++ b/solution.py
@@ -22,8 +22,8 @@
 NMSG = RCH * QCH
 PER = QCH // 2
 STEPS = 2 * RCH
-HOP = 3
-LAG = 5
+HOP = 4
+LAG = 6
 LAG_Y = 6
 SLOTS = 3
 

time: 79.1 us -> 78.3 us (0.990)
  Pallas kernels: 78.2 us -> 77.4 us
where the time goes in v7:
time: 78.3 us; the launch traced here: 78.1 us
  Pallas kernels  77.4 us (99%)
    pallas_call x1, Pallas kernels, block(): pl.pallas_call(functools.partial(block_kernel, positions=positions, scale...  75.7 us
    pallas_call x1, Pallas kernels, emit(): pl.pallas_call(emit_kernel, out_shape=tuple((jax.ShapeDtypeStruct(v.shape...  1.76 us

profile of v7, /device:TPU:0, one launch (start us, length us, event | category | flops | bytes accessed | tf_op | source)
XLA Modules:
  0.0 78.1 jit_solution(14712221151819532133)
XLA Ops:
  0.6 75.7 %block.1 = (bf16[256,6144]{1,0:T(8,128)(2,1)S(1)}, bf16[512,128]{1,0:T(8,128)(2,1)S(1)}, bf16[512,128]{1,0:T(8,128)(2,1)S(1)}) custom-call(s32[2,128]{1,0:T(2,128)} %bitcast.11, f32[1,128]{1,0:T(1,128)} %constant.2.clone.freq_hbm, bf16[48,128]{1,0:T(8,128)(2,1)} %bitcast.9, bf16[48,128]{1,0:T(8,128)(2,1)} %bitcast.10, bf16[256,6144]{1,0:T(8,128)(2,1)} %x_hbm.1, ...), custom_call_target="tpu_custom_call" | custom-call | tf_op jit(solution)/shard_map/block/pallas_call | solution.py:498
  76.3 1.8 %emit.1 = (bf16[256,6144]{1,0:T(8,128)(2,1)}, bf16[512,128]{1,0:T(8,128)(2,1)}, bf16[512,128]{1,0:T(8,128)(2,1)}) custom-call(bf16[256,6144]{1,0:T(8,128)(2,1)S(1)} %get-tuple-element.9.refs_0_, bf16[512,128]{1,0:T(8,128)(2,1)S(1)} %get-tuple-element.10.refs_1_, bf16[512,128]{1,0:T(8,128)(2,1)S(1)} %get-tuple-element.11.refs_2_), custom_call_target="tpu_custom_call" | custom-call | tf_op jit(solution)/shard_map/emit/pallas_call | solution.py:540

commit v8 on v7

--- a/solution.py
+++ b/solution.py
@@ -330,6 +330,8 @@
     lag = LAG * (2 - hops)
     lag_y = lag + LAG_Y
     start = 2 * QCH + HOP * hops
+    hops_p = 3 - u - 2 * ((3 - u) // 3)
+    start_p = 2 * QCH + HOP * hops_p + LAG * (2 - hops_p) + LAG_Y + 4
 
     def tick(t, carry):
         i, r6 = t // PER, t // QCH
@@ -344,9 +346,10 @@
                 k_copy(i + SLOTS).start()
                 v_copy(i + SLOTS).start()
 
-            @pl.when(i < QCH)
-            def _():
-                w_copy(i).start()
+            @pl.when((i >= 2) & (i < 5))
+            def _():
+                w_copy(2 * i - 4).start()
+                w_copy(2 * i - 3).start()
 
         @pl.when((t % QCH == PER + 1) & (t < NMSG))
         def _():
@@ -433,18 +436,18 @@
             fe(jy).start()
             convert(yo, c, jy)
 
+        jp = t - start_p
+
+        @pl.when((jp >= 0) & (jp < NMSG))
+        def _():
+            fd_in(jp).wait_recv()
+            fe_in(jp).wait_recv()
+            convert(y, co, jp)
+            convert(yo, co, jp)
+
         return carry
 
-    lax.fori_loop(0, start + NMSG + lag_y, tick, 0)
-
-    def last(j, carry):
-        fd_in(j).wait_recv()
-        fe_in(j).wait_recv()
-        convert(y, co, j)
-        convert(yo, co, j)
-        return carry
-
-    lax.fori_loop(0, NMSG, last, 0)
+    lax.fori_loop(0, 2 * QCH + 2 * LAG + LAG_Y + 4 + NMSG, tick, 0)
 
     def drain(j, carry):
         @pl.when(u < 2)

time: 78.3 us -> 78.4 us (level)
  no operation moved by 1% of the time
where the time goes in v8:
time: 78.4 us; the launch traced here: 78.1 us
  Pallas kernels  77.5 us (99%)
    pallas_call x1, Pallas kernels, block(): pl.pallas_call(functools.partial(block_kernel, positions=positions, scale...  75.7 us
    pallas_call x1, Pallas kernels, emit(): pl.pallas_call(emit_kernel, out_shape=tuple((jax.ShapeDtypeStruct(v.shape...  1.76 us

profile of v8, /device:TPU:0, one launch (start us, length us, event | category | flops | bytes accessed | tf_op | source)
XLA Modules:
  0.0 78.1 jit_solution(16699497013559339956)
XLA Ops:
  0.6 75.7 %block.1 = (bf16[256,6144]{1,0:T(8,128)(2,1)S(1)}, bf16[512,128]{1,0:T(8,128)(2,1)S(1)}, bf16[512,128]{1,0:T(8,128)(2,1)S(1)}) custom-call(s32[2,128]{1,0:T(2,128)} %bitcast.11, f32[1,128]{1,0:T(1,128)} %constant.2.clone.freq_hbm, bf16[48,128]{1,0:T(8,128)(2,1)} %bitcast.9, bf16[48,128]{1,0:T(8,128)(2,1)} %bitcast.10, bf16[256,6144]{1,0:T(8,128)(2,1)} %x_hbm.1, ...), custom_call_target="tpu_custom_call" | custom-call | tf_op jit(solution)/shard_map/block/pallas_call | solution.py:501
  76.3 1.8 %emit.1 = (bf16[256,6144]{1,0:T(8,128)(2,1)}, bf16[512,128]{1,0:T(8,128)(2,1)}, bf16[512,128]{1,0:T(8,128)(2,1)}) custom-call(bf16[256,6144]{1,0:T(8,128)(2,1)S(1)} %get-tuple-element.9.refs_0_, bf16[512,128]{1,0:T(8,128)(2,1)S(1)} %get-tuple-element.10.refs_1_, bf16[512,128]{1,0:T(8,128)(2,1)S(1)} %get-tuple-element.11.refs_2_), custom_call_target="tpu_custom_call" | custom-call | tf_op jit(solution)/shard_map/emit/pallas_call | solution.py:543

commit v9 on v8

--- a/solution.py
+++ b/solution.py
@@ -113,6 +113,8 @@
     def share(slot):
         return remote(xs.at[slot], xr.at[slot], s_xs.at[slot], r_xs.at[slot], partner)
 
+    for h in range(12, 16):
+        q_ref[pl.ds(h, rows, stride=16), :] = jnp.zeros((rows, 128), F32)
     for copy in small:
         copy.wait()
     for k in range(tiles):
@@ -178,13 +180,13 @@
             dst = kf if slot == 6 else vf
             dst[pl.ds(core, rows, stride=2), :] = v
 
-    for h in range(12, 16):
-        q_ref[pl.ds(h, rows, stride=16), :] = jnp.zeros((rows, 128), F32)
-
     for g in range(2):
         for n in range(4):
             for copy in ([q_copy(n)] if g == 0 else g_copies(n)):
                 copy.wait()
+        if g == 1:
+            for slot in range(4):
+                spread_out(slot, c, xs[slot])
         parts = [jnp.dot(hbuf[:, n * depth:(n + 1) * depth], wbuf[4 * g + n], preferred_element_type=F32) for n in range(4)]
         acc_ref[...] = (parts[0] + parts[1]) + (parts[2] + parts[3])
         if g == 0:
@@ -193,8 +195,8 @@
             v = acc_ref[:, (slot % 4) * 128:(slot % 4 + 1) * 128]
             xs[slot] = rotate(v) if slot < 7 else v
             share(slot).start()
-        for slot in range(4 * g, 4 * g + 4):
-            spread_out(slot, c, xs[slot])
+    for slot in range(4, 8):
+        spread_out(slot, c, xs[slot])
     for slot in range(8):
         share(slot).wait_recv()
         spread_out(slot, co, xr[slot])
@@ -346,10 +348,9 @@
                 k_copy(i + SLOTS).start()
                 v_copy(i + SLOTS).start()
 
-            @pl.when((i >= 2) & (i < 5))
-            def _():
-                w_copy(2 * i - 4).start()
-                w_copy(2 * i - 3).start()
+            @pl.when(i < QCH)
+            def _():
+                w_copy(i).start()
 
         @pl.when((t % QCH == PER + 1) & (t < NMSG))
         def _():

time: 78.4 us -> 78.6 us (level)
  no operation moved by 1% of the time
where the time goes in v9:
time: 78.6 us; the launch traced here: 78.4 us
  Pallas kernels  77.7 us (99%)
    pallas_call x1, Pallas kernels, block(): pl.pallas_call(functools.partial(block_kernel, positions=positions, scale...  76 us
    pallas_call x1, Pallas kernels, emit(): pl.pallas_call(emit_kernel, out_shape=tuple((jax.ShapeDtypeStruct(v.shape...  1.76 us

profile of v9, /device:TPU:0, one launch (start us, length us, event | category | flops | bytes accessed | tf_op | source)
XLA Modules:
  0.0 78.4 jit_solution(17874700609508678948)
XLA Ops:
  0.6 76.0 %block.1 = (bf16[256,6144]{1,0:T(8,128)(2,1)S(1)}, bf16[512,128]{1,0:T(8,128)(2,1)S(1)}, bf16[512,128]{1,0:T(8,128)(2,1)S(1)}) custom-call(s32[2,128]{1,0:T(2,128)} %bitcast.11, f32[1,128]{1,0:T(1,128)} %constant.2.clone.freq_hbm, bf16[48,128]{1,0:T(8,128)(2,1)} %bitcast.9, bf16[48,128]{1,0:T(8,128)(2,1)} %bitcast.10, bf16[256,6144]{1,0:T(8,128)(2,1)} %x_hbm.1, ...), custom_call_target="tpu_custom_call" | custom-call | tf_op jit(solution)/shard_map/block/pallas_call | solution.py:502
  76.6 1.8 %emit.1 = (bf16[256,6144]{1,0:T(8,128)(2,1)}, bf16[512,128]{1,0:T(8,128)(2,1)}, bf16[512,128]{1,0:T(8,128)(2,1)}) custom-call(bf16[256,6144]{1,0:T(8,128)(2,1)S(1)} %get-tuple-element.9.refs_0_, bf16[512,128]{1,0:T(8,128)(2,1)S(1)} %get-tuple-element.10.refs_1_, bf16[512,128]{1,0:T(8,128)(2,1)S(1)} %get-tuple-element.11.refs_2_), custom_call_target="tpu_custom_call" | custom-call | tf_op jit(solution)/shard_map/emit/pallas_call | solution.py:544

commit v10 on v9

--- a/solution.py
+++ b/solution.py
@@ -22,7 +22,7 @@
 NMSG = RCH * QCH
 PER = QCH // 2
 STEPS = 2 * RCH
-HOP = 4
+HOP = 5
 LAG = 6
 LAG_Y = 6
 SLOTS = 3
@@ -348,9 +348,10 @@
                 k_copy(i + SLOTS).start()
                 v_copy(i + SLOTS).start()
 
-            @pl.when(i < QCH)
-            def _():
-                w_copy(i).start()
+            @pl.when((i >= 2) & (i < 5))
+            def _():
+                w_copy(2 * i - 4).start()
+                w_copy(2 * i - 3).start()
 
         @pl.when((t % QCH == PER + 1) & (t < NMSG))
         def _():

time: 78.6 us -> 78.9 us (level)
  no operation moved by 1% of the time
where the time goes in v10:
time: 78.9 us; the launch traced here: 78.6 us
  Pallas kernels  78 us (99%)
    pallas_call x1, Pallas kernels, block(): pl.pallas_call(functools.partial(block_kernel, positions=positions, scale...  76.2 us
    pallas_call x1, Pallas kernels, emit(): pl.pallas_call(emit_kernel, out_shape=tuple((jax.ShapeDtypeStruct(v.shape...  1.76 us

profile of v10, /device:TPU:0, one launch (start us, length us, event | category | flops | bytes accessed | tf_op | source)
XLA Modules:
  0.0 78.6 jit_solution(14221677829042846009)
XLA Ops:
  0.6 76.2 %block.1 = (bf16[256,6144]{1,0:T(8,128)(2,1)S(1)}, bf16[512,128]{1,0:T(8,128)(2,1)S(1)}, bf16[512,128]{1,0:T(8,128)(2,1)S(1)}) custom-call(s32[2,128]{1,0:T(2,128)} %bitcast.11, f32[1,128]{1,0:T(1,128)} %constant.2.clone.freq_hbm, bf16[48,128]{1,0:T(8,128)(2,1)} %bitcast.9, bf16[48,128]{1,0:T(8,128)(2,1)} %bitcast.10, bf16[256,6144]{1,0:T(8,128)(2,1)} %x_hbm.1, ...), custom_call_target="tpu_custom_call" | custom-call | tf_op jit(solution)/shard_map/block/pallas_call | solution.py:503
  76.9 1.8 %emit.1 = (bf16[256,6144]{1,0:T(8,128)(2,1)}, bf16[512,128]{1,0:T(8,128)(2,1)}, bf16[512,128]{1,0:T(8,128)(2,1)}) custom-call(bf16[256,6144]{1,0:T(8,128)(2,1)S(1)} %get-tuple-element.9.refs_0_, bf16[512,128]{1,0:T(8,128)(2,1)S(1)} %get-tuple-element.10.refs_1_, bf16[512,128]{1,0:T(8,128)(2,1)S(1)} %get-tuple-element.11.refs_2_), custom_call_target="tpu_custom_call" | custom-call | tf_op jit(solution)/shard_map/emit/pallas_call | solution.py:545

commit v11 on v7

--- a/solution.py
+++ b/solution.py
@@ -344,9 +344,10 @@
                 k_copy(i + SLOTS).start()
                 v_copy(i + SLOTS).start()
 
-            @pl.when(i < QCH)
-            def _():
-                w_copy(i).start()
+            @pl.when((i >= 2) & (i < 5))
+            def _():
+                w_copy(2 * i - 4).start()
+                w_copy(2 * i - 3).start()
 
         @pl.when((t % QCH == PER + 1) & (t < NMSG))
         def _():

time: 78.3 us -> 78.3 us (level)
  no operation moved by 1% of the time
where the time goes in v11:
time: 78.3 us; the launch traced here: 78 us
  Pallas kernels  77.4 us (99%)
    pallas_call x1, Pallas kernels, block(): pl.pallas_call(functools.partial(block_kernel, positions=positions, scale...  75.6 us
    pallas_call x1, Pallas kernels, emit(): pl.pallas_call(emit_kernel, out_shape=tuple((jax.ShapeDtypeStruct(v.shape...  1.76 us

profile of v11, /device:TPU:0, one launch (start us, length us, event | category | flops | bytes accessed | tf_op | source)
XLA Modules:
  0.0 78.0 jit_solution(4753629849873221669)
XLA Ops:
  0.6 75.6 %block.1 = (bf16[256,6144]{1,0:T(8,128)(2,1)S(1)}, bf16[512,128]{1,0:T(8,128)(2,1)S(1)}, bf16[512,128]{1,0:T(8,128)(2,1)S(1)}) custom-call(s32[2,128]{1,0:T(2,128)} %bitcast.11, f32[1,128]{1,0:T(1,128)} %constant.2.clone.freq_hbm, bf16[48,128]{1,0:T(8,128)(2,1)} %bitcast.9, bf16[48,128]{1,0:T(8,128)(2,1)} %bitcast.10, bf16[256,6144]{1,0:T(8,128)(2,1)} %x_hbm.1, ...), custom_call_target="tpu_custom_call" | custom-call | tf_op jit(solution)/shard_map/block/pallas_call | solution.py:499
  76.3 1.8 %emit.1 = (bf16[256,6144]{1,0:T(8,128)(2,1)}, bf16[512,128]{1,0:T(8,128)(2,1)}, bf16[512,128]{1,0:T(8,128)(2,1)}) custom-call(bf16[256,6144]{1,0:T(8,128)(2,1)S(1)} %get-tuple-element.9.refs_0_, bf16[512,128]{1,0:T(8,128)(2,1)S(1)} %get-tuple-element.10.refs_1_, bf16[512,128]{1,0:T(8,128)(2,1)S(1)} %get-tuple-element.11.refs_2_), custom_call_target="tpu_custom_call" | custom-call | tf_op jit(solution)/shard_map/emit/pallas_call | solution.py:541

commit v12 on v11

--- a/solution.py
+++ b/solution.py
@@ -22,7 +22,7 @@
 NMSG = RCH * QCH
 PER = QCH // 2
 STEPS = 2 * RCH
-HOP = 4
+HOP = 3
 LAG = 6
 LAG_Y = 6
 SLOTS = 3

time: 78.3 us -> 78.7 us (level)
  no operation moved by 1% of the time
where the time goes in v12:
time: 78.7 us; the launch traced here: 78.4 us
  Pallas kernels  77.8 us (99%)
    pallas_call x1, Pallas kernels, block(): pl.pallas_call(functools.partial(block_kernel, positions=positions, scale...  76 us
    pallas_call x1, Pallas kernels, emit(): pl.pallas_call(emit_kernel, out_shape=tuple((jax.ShapeDtypeStruct(v.shape...  1.76 us

profile of v12, /device:TPU:0, one launch (start us, length us, event | category | flops | bytes accessed | tf_op | source)
XLA Modules:
  0.0 78.4 jit_solution(9301301555947745602)
XLA Ops:
  0.6 76.0 %block.1 = (bf16[256,6144]{1,0:T(8,128)(2,1)S(1)}, bf16[512,128]{1,0:T(8,128)(2,1)S(1)}, bf16[512,128]{1,0:T(8,128)(2,1)S(1)}) custom-call(s32[2,128]{1,0:T(2,128)} %bitcast.11, f32[1,128]{1,0:T(1,128)} %constant.2.clone.freq_hbm, bf16[48,128]{1,0:T(8,128)(2,1)} %bitcast.9, bf16[48,128]{1,0:T(8,128)(2,1)} %bitcast.10, bf16[256,6144]{1,0:T(8,128)(2,1)} %x_hbm.1, ...), custom_call_target="tpu_custom_call" | custom-call | tf_op jit(solution)/shard_map/block/pallas_call | solution.py:499
  76.7 1.8 %emit.1 = (bf16[256,6144]{1,0:T(8,128)(2,1)}, bf16[512,128]{1,0:T(8,128)(2,1)}, bf16[512,128]{1,0:T(8,128)(2,1)}) custom-call(bf16[256,6144]{1,0:T(8,128)(2,1)S(1)} %get-tuple-element.9.refs_0_, bf16[512,128]{1,0:T(8,128)(2,1)S(1)} %get-tuple-element.10.refs_1_, bf16[512,128]{1,0:T(8,128)(2,1)S(1)} %get-tuple-element.11.refs_2_), custom_call_target="tpu_custom_call" | custom-call | tf_op jit(solution)/shard_map/emit/pallas_call | solution.py:541
